TPU v7x, 1024 devices: a whole 4x8x16 slice. The times are simulated.
1024 devices in a mesh: row: 16 (over y, core), col: 64 (over x, z).
Axes of the slice: x: 4, y: 8, z: 16, core: 2. Of those that a mesh axis runs over, the one named last changes fastest.
Arguments:
- matrix: float32 [16384, 16384], P('row', 'col'), may hold values from -1 to 4, as said below
Outputs:
- reduced: float32 [16384, 16384], P('row', 'col')
Inputs may be any that keep to these rules, and one draw needn't show every extreme that they name: matrix is symmetric; its diagonal entries lie between 1 and 3 up to entries of size about 16384^-1/2 that every entry carries; entries at distance 256 from the diagonal with the smaller index under 2 * 256 carry an added 2.
All inputs are finite; a program needn't handle non-finite values.
Results may differ from a plain program's by a relative error of at most 0.00019.
Values sent between devices are 32-bit elements; how exact they have to be, the bound alone decides.
No kernel may reach another device: no remote copies, remote signals or barrier semaphores. Data moves between devices by JAX's collectives and lax.ppermute only.
A program may use at most 32 MiB of HBM per device.

v0:
```python
import jax
import jax.numpy as jnp
from jax import lax
from jax.sharding import Mesh
from jax.sharding import PartitionSpec as P

COL = ("col_0", "col_1")


def from_root(x, axis, root):
    return lax.dynamic_index_in_dim(lax.all_gather(x, axis), root, 0, keepdims=False)


def spread(x, axes, root):
    x = jnp.where(lax.axis_index(axes) == root, x, jnp.zeros_like(x))
    for axis in axes:
        x = lax.psum(x, axis)
    return x


def in_one(arrays, axis):
    ravelled, at, outs = (jnp.concatenate([a.reshape(-1) for a in arrays]), 0, [])
    subtotal = lax.psum(ravelled, axis)
    for a in arrays:
        outs.append(subtotal[at : at + a.size].reshape(a.shape))
        at += a.size
    return tuple(outs)


def in_blocks(x, dim, devices):
    lengths = x.shape
    tiles = x.reshape(*lengths[:dim], devices, lengths[dim] // devices, *lengths[dim + 1 :])
    return jnp.moveaxis(tiles, dim, 0)


def sum_at_owner(x, axis, dim):
    devices = lax.axis_size(axis)
    tiles = lax.all_to_all(in_blocks(x, dim, devices), axis, 0, 0, tiled=True)
    return jnp.sum(tiles, axis=0)


def joined_along(tiles, dim):
    lengths = list(tiles.shape[1:])
    lengths[dim] *= tiles.shape[0]
    return jnp.moveaxis(tiles, 0, dim).reshape(lengths)


def all_blocks(x, axes, turns):
    tiles = x
    for k in turns:
        tiles = lax.all_gather(tiles, axes[k])
    done = turns[::-1]
    back = [done.index(k) for k in range(len(axes))]
    tiles = tiles.transpose(*back, *range(len(axes), tiles.ndim))
    return tiles.reshape(-1, *x.shape)


def gathered_by_axis(x, axes, turns, dim):
    return joined_along(all_blocks(x, axes, turns), dim)


def over_pieces(x, axis):
    tiles = lax.all_gather(x, axis)
    return tiles.sum(axis=0)


def product(left, right):
    return jnp.dot(left, right, precision=lax.Precision.HIGHEST, preferred_element_type=jnp.float32)


def left_product(left, right):
    return lax.dot_general(
        left,
        right,
        (((0,), (0,)), ((), ())),
        precision=lax.Precision.HIGHEST,
        preferred_element_type=jnp.float32,
    )


def right_product(left, right):
    return lax.dot_general(
        left,
        right,
        (((1,), (1,)), ((), ())),
        precision=lax.Precision.HIGHEST,
        preferred_element_type=jnp.float32,
    )


def factor_inverse(kmat):
    cholesky_low = jnp.linalg.cholesky(left_product(kmat, kmat))
    halfway = lax.linalg.triangular_solve(cholesky_low, kmat.T, left_side=True, lower=True)
    return lax.linalg.triangular_solve(
        cholesky_low, halfway, left_side=True, lower=True, transpose_a=True
    )


def transpose_rows(local, row_id, col_id, row_count, panel_width):
    root = col_id * panel_width // row_count
    offset = jnp.clip(col_id * panel_width - row_id * row_count, 0, row_count - panel_width)
    piece = lax.dynamic_slice_in_dim(local, offset, panel_width, 0)
    return from_root(piece, "row", root)


def per_device(matrix):
    row_count, panel_width = matrix.shape
    row_id = lax.axis_index("row")
    col_id = lax.axis_index(COL)
    global_rows = row_id * row_count + lax.iota(jnp.int32, row_count)
    columns = lax.iota(jnp.int32, panel_width)
    identity = jnp.eye(panel_width, dtype=jnp.float32)
    current = matrix
    sign = 1.0
    panel = spread(current, COL, 0)
    panel = jnp.where((global_rows >= panel_width)[:, None], panel, 0.0)
    offset = jnp.clip(panel_width - row_id * row_count, 0, row_count - panel_width)
    owner = (row_id == panel_width // row_count).astype(jnp.float32)
    top_local = lax.dynamic_slice_in_dim(panel, offset, panel_width, 0) * owner
    gram, top = in_one((left_product(panel, panel), top_local), "row")
    cholesky_low = jnp.linalg.cholesky(gram)
    ortho = lax.linalg.triangular_solve(
        cholesky_low, panel, left_side=False, lower=True, transpose_a=True
    )
    top_q = lax.linalg.triangular_solve(
        cholesky_low, top, left_side=False, lower=True, transpose_a=True
    )
    tfac = factor_inverse(identity + sign * top_q)
    unit = (global_rows[:, None] - panel_width == columns[None, :]).astype(jnp.float32)
    refl_rows = ortho + sign * unit
    refl_cols = transpose_rows(refl_rows, row_id, col_id, row_count, panel_width)
    x_share = sum_at_owner(product(current, refl_cols), COL, 0)
    x_rows = gathered_by_axis(x_share, COL, (0, 1), 0)
    y_local = left_product(refl_rows, x_rows)
    y_full = over_pieces(y_local, "row")
    middle = product(product(tfac.T, y_full), tfac)
    w_rows = product(x_rows, tfac) - 0.5 * product(refl_rows, middle)
    w_cols = transpose_rows(w_rows, row_id, col_id, row_count, panel_width)
    current = current - right_product(w_rows, refl_cols) - right_product(refl_rows, w_cols)
    return current


def solution(mesh):
    torus = Mesh(mesh.devices.reshape(mesh.shape["row"], 4, 16), ("row", "col_0", "col_1"))
    in_specs = (P("row", COL),)
    out_specs = P("row", COL)
    return jax.shard_map(
        per_device, mesh=torus, in_specs=in_specs, out_specs=out_specs, check_vma=False
    )
```

profile of v0, /device:TPU:1, one launch (start us, length us, event | category | flops | bytes accessed | tf_op | source)
XLA Modules:
  0.0 795.4 jit_solution(18109106941875629080)
XLA Ops:
  6.5 2.3 broadcast_select_fusion.1
  8.9 75.3 %all-reduce.5.cloned.1.call-done = f32[1024,256]{1,0:T(8,128)} async-done(((f32[1024,256]{1,0:T(8,128)}), f32[1024,256]{1,0:T(8,128)}) %all-reduce.5.cloned.1.call-update) | async-done | bytes 1048592 | tf_op jit(solution)/shard_map/psum | solution.py:17
  84.3 141.8 %all-reduce.7.cloned.1.call-done = f32[1024,256]{1,0:T(8,128)} async-done(((f32[1024,256]{1,0:T(8,128)}), f32[1024,256]{1,0:T(8,128)}) %all-reduce.7.cloned.1.call-update) | async-done | bytes 1048592 | tf_op jit(solution)/shard_map/psum | solution.py:17
  231.2 132.1 %all-reduce.9.cloned.1.call-done = f32[131072]{0:T(1024)} async-done(((f32[131072]{0:T(1024)}), f32[131072]{0:T(1024)}) %all-reduce.9.cloned.1.call-update) | async-done | bytes 524304 | tf_op jit(solution)/shard_map/psum | solution.py:23
  365.3 11.7 %cholesky.130 = f32[128,128]{1,0:T(8,128)S(1)} custom-call(f32[128,128]{1,0:T(8,128)S(1)} %cholesky.194), custom_call_target="Cholesky" | custom-call | tf_op jit(solution)/shard_map/jit(cholesky)/cholesky | solution.py:121
  377.1 9.8 %custom-call.21 = f32[1,128,128]{1,2,0:T(8,128)S(1)} custom-call(f32[1,128,128]{2,1,0:T(8,128)S(1)} %get-tuple-element.51), custom_call_target="InvertDiagBlocksLowerTriangular" | custom-call | tf_op jit(solution)/shard_map/jit(cholesky)/cholesky | solution.py:121
  387.4 11.7 %cholesky.147 = f32[128,128]{1,0:T(8,128)S(1)} custom-call(f32[128,128]{1,0:T(8,128)S(1)} %convolution_subtract_fusion.7), custom_call_target="Cholesky" | custom-call | tf_op jit(solution)/shard_map/jit(cholesky)/cholesky | solution.py:121
  401.2 4.2 while.2
  405.4 19.7 %custom-call.18 = f32[2,128,128]{1,2,0:T(8,128)S(1)} custom-call(f32[2,128,128]{2,1,0:T(8,128)S(1)} %get-tuple-element.13), custom_call_target="InvertDiagBlocksLowerTriangular" | custom-call | tf_op jit(solution)/shard_map/triangular_solve | solution.py:122
  428.4 51.3 %all-gather.10.cloned.1.call-done = f32[4096,256]{0,1:T(8,128)} async-done(((f32[256,256]{0,1:T(8,128)}), f32[4096,256]{0,1:T(8,128)}) %all-gather.10.cloned.1.call-update) | async-done | bytes 4194320 | tf_op jit(solution)/shard_map/all_gather | solution.py:11
  479.7 4.0 copy.18
  484.7 2.0 convolution_bitcast_fusion
  488.3 66.6 %all_to_all.5 = f32[64,16,256]{2,1,0:T(8,128)} all-to-all(f32[64,16,256]{2,1,0:T(8,128)S(1)} %bitcast.118), channel_id=1, replica_groups=mesh['row'=16,'col_0'=4,'col_1'=16] {'col_0','col_1'}, dimensions={0} | all-to-all | bytes 2097152 | tf_op jit(solution)/shard_map/all_to_all | solution.py:38
  556.2 10.1 %all-gather.1 = f32[64,256]{1,0:T(8,128)} all-gather(f32[16,256]{1,0:T(8,128)S(1)} %reduce_sum.18), channel_id=3, replica_groups=mesh['row'=16,'col_0'=4,'col_1'=16] {'col_0'}, dimensions={0}, use_global_device_ids=true | all-gather | bytes 81920 | tf_op jit(solution)/shard_map/all_gather | solution.py:51
  566.3 60.0 %all-gather.12.cloned.1.call-done = f32[64,16,256]{2,1,0:T(8,128)} async-done(((f32[4,16,256]{2,1,0:T(8,128)}), f32[64,16,256]{2,1,0:T(8,128)}) %all-gather.12.cloned.1.call-update) | async-done | bytes 1048592 | tf_op jit(solution)/shard_map/all_gather | solution.py:51
  638.7 11.7 %cholesky.164 = f32[128,128]{1,0:T(8,128)S(1)} custom-call(f32[128,128]{1,0:T(8,128)S(1)} %cholesky.197), custom_call_target="Cholesky" | custom-call | tf_op jit(solution)/shard_map/jit(cholesky)/cholesky | solution.py:92
  651.0 10.4 %custom-call.22 = f32[1,128,128]{1,2,0:T(8,128)} custom-call(f32[1,128,128]{2,1,0:T(8,128)S(1)} %get-tuple-element.47), custom_call_target="InvertDiagBlocksLowerTriangular" | custom-call | tf_op jit(solution)/shard_map/jit(cholesky)/cholesky | solution.py:92
  665.1 13.2 %cholesky.181 = f32[128,128]{1,0:T(8,128)} custom-call(f32[128,128]{1,0:T(8,128)} %convolution_subtract_fusion.6), custom_call_target="Cholesky" | custom-call | tf_op jit(solution)/shard_map/jit(cholesky)/cholesky | solution.py:92
  683.5 5.4 while.3
  688.9 21.1 %custom-call.19 = f32[2,128,128]{1,2,0:T(8,128)} custom-call(f32[2,128,128]{2,1,0:T(8,128)} %get-tuple-element.21), custom_call_target="InvertDiagBlocksLowerTriangular" | custom-call | tf_op jit(solution)/shard_map/triangular_solve | solution.py:94
  719.5 2.5 reduce_sum.19
  723.0 3.0 fusion
  728.8 55.3 %all-gather.16.cloned.1.call-done = f32[4096,256]{1,0:T(8,128)} async-done(((f32[256,256]{1,0:T(8,128)}), f32[4096,256]{1,0:T(8,128)}) %all-gather.16.cloned.1.call-update) | async-done | bytes 4194320 | tf_op jit(solution)/shard_map/all_gather | solution.py:11
  784.2 4.1 convolution_subtract_fusion
  (111 shorter events, 58.3 us)
Async XLA Ops:
  6.5 77.7 %all-reduce.5.cloned.1.call-start = ((), (), s32[]{:S(2)}) async-start(), calls=%async_computation.1 | async-start | bytes 2097152 | tf_op jit(solution)/shard_map/psum | solution.py:17
  8.8 217.3 %all-reduce.7.cloned.1.call-start = ((), (), s32[]{:S(2)}) async-start(), calls=%async_computation.2 | async-start | bytes 2097152 | tf_op jit(solution)/shard_map/psum | solution.py:17
  84.2 279.1 %all-reduce.9.cloned.1.call-start = ((), (), s32[]{:S(2)}) async-start(), calls=%async_computation.3 | async-start | bytes 1048576 | tf_op jit(solution)/shard_map/psum | solution.py:23
  230.6 249.1 %all-gather.10.cloned.1.call-start = ((), (), s32[]{:S(2)}) async-start(), calls=%async_computation.4 | async-start | bytes 4456448 | tf_op jit(solution)/shard_map/all_gather | solution.py:11
  425.1 54.6 %copy-start.9 = (f32[2,128,128]{1,2,0:T(8,128)}, f32[2,128,128]{1,2,0:T(8,128)S(1)}, u32[]{:S(2)}) copy-start(f32[2,128,128]{1,2,0:T(8,128)S(1)} %custom-call.18) | copy-start | bytes 393220
  428.4 197.9 %all-gather.12.cloned.1.call-start = ((), (), s32[]{:S(2)}) async-start(), calls=%async_computation.5 | async-start | bytes 1114112 | tf_op jit(solution)/shard_map/all_gather | solution.py:51
  479.7 5.0 copy-start
  484.0 0.7 copy-start.1
  566.3 153.2 %all-gather.14.cloned.1.call-start = ((), (), s32[]{:S(2)}) async-start(), calls=%async_computation.6 | async-start | bytes 4456448 | tf_op jit(solution)/shard_map/all_gather | solution.py:63
  629.4 154.8 %all-gather.16.cloned.1.call-start = ((), (), s32[]{:S(2)}) async-start(), calls=%async_computation.7 | async-start | bytes 4456448 | tf_op jit(solution)/shard_map/all_gather | solution.py:11
  635.1 0.6 copy-start.6
  637.9 0.7 copy-start.8
  650.4 0.6 copy-start.10
  679.8 2.0 copy-start.7
  688.9 23.5 %copy-start.5 = (f32[256,256]{1,0:T(8,128)}, f32[256,256]{1,0:T(8,128)S(1)}, u32[]{:S(2)}) copy-start(f32[256,256]{1,0:T(8,128)S(1)} %get-tuple-element.160) | copy-start | bytes 786436
  716.9 0.6 copy-start.3
  719.5 2.5 copy-start.4
  719.5 7.4 copy-start.2
Sparse Core Ops, SparseCore 0:
  9.7 74.4 all-reduce.4
  86.5 139.5 all-reduce.6
  230.7 132.5 all-reduce.8
  428.5 51.1 all-gather.9
  566.4 59.8 all-gather.11
  629.5 57.4 all-gather.13
  727.0 57.1 all-gather.15
where the time goes:
time: 799 us; the launch traced here: 795 us
  waiting for transfers between devices  516 us (65%)
  other arithmetic  124 us (16%)
  blocking collectives  76.6 us (10%)
  matrix products  33.2 us (4%)
  local copies, waits for them, and re-layouts  27.5 us (3%)
  between operations  16.8 us (2%)
    psum x2, waiting for transfers between devices, spread(): x = lax.psum(x, axis)  217 us
    psum x1, waiting for transfers between devices, in_one(): subtotal = lax.psum(ravelled, axis)  132 us
    all_gather x2, waiting for transfers between devices, from_root(): lax.all_gather(x, axis)  107 us
    all_to_all x1, blocking collectives, sum_at_owner(): tiles = lax.all_to_all(in_blocks(x, dim, devices), axis, 0, 0, tiled=True)  66.6 us
    all_gather x1, waiting for transfers between devices, all_blocks(): tiles = lax.all_gather(tiles, axes[k])  60 us
    another operation x7, other arithmetic, factor_inverse(): cholesky_low = jnp.linalg.cholesky(left_product(kmat, kmat))  37.6 us
    another operation x6, other arithmetic, per_device(): cholesky_low = jnp.linalg.cholesky(gram)  34 us
    another operation x2, other arithmetic, factor_inverse(): lax.linalg.triangular_solve(cholesky_low, halfway, left_side=True, lower=...  22.1 us
  transfers between devices with their start and end apart: 7, of which 6 were waited for; matrix products, arithmetic and copies ran while one was open for 11% of the time, Pallas kernels for 0%

commit v1 on v0

v1 whole, which is shorter than its diff:
```python
import jax
import jax.numpy as jnp
from jax import lax
from jax.experimental import pallas as pl
from jax.experimental.pallas import tpu as pltpu
from jax.sharding import Mesh
from jax.sharding import PartitionSpec as P

ROW = ("y", "core")
COL = ("x", "z")
EVERY = ROW + COL
SIGN = 1.0


def dot(left, right, dims):
    return lax.dot_general(
        left,
        right,
        (dims, ((), ())),
        precision=lax.Precision.HIGHEST,
        preferred_element_type=jnp.float32,
    )


def mm(left, right):
    return dot(left, right, ((1,), (0,)))


def tn(left, right):
    return dot(left, right, ((0,), (0,)))


def nt(left, right):
    return dot(left, right, ((1,), (1,)))


def exchange(tiles, axis):
    return lax.all_to_all(tiles, axis, 0, 0, tiled=True)


def to_all(piece, axis):
    n = lax.axis_size(axis)
    return exchange(jnp.broadcast_to(piece[None], (n, *piece.shape)), axis)


def invert_half(m_ref, c_ref):
    n = m_ref.shape[0]
    lanes = lax.broadcasted_iota(jnp.int32, (n, n), 1)
    subs = lax.broadcasted_iota(jnp.int32, (n, n), 0)
    lane_row = lax.broadcasted_iota(jnp.int32, (1, n), 1)

    def step(k, carry):
        m = m_ref[...]
        hit = lanes == k
        col = jnp.sum(jnp.where(hit, m, 0.0), axis=1, keepdims=True)
        c_ref[...] = jnp.broadcast_to(col, (n, n))
        pivot = c_ref[pl.ds(k, 1), :]
        row = jnp.where(lane_row == k, 1.0, m_ref[pl.ds(k, 1), :]) / pivot
        rest = jnp.where(hit, 0.0, m) - c_ref[...] * row
        m_ref[...] = jnp.where(subs == k, row, rest)
        return carry

    lax.fori_loop(0, n, step, 0)


def inverse_kernel(a_ref, out_ref, m_ref, c_ref):
    h = a_ref.shape[0] // 2
    a12 = a_ref[:h, h:]
    a21 = a_ref[h:, :h]
    m_ref[...] = a_ref[:h, :h]
    invert_half(m_ref, c_ref)
    t11 = m_ref[...]
    right = mm(t11, a12)
    left = mm(a21, t11)
    m_ref[...] = a_ref[h:, h:] - mm(a21, right)
    invert_half(m_ref, c_ref)
    t22 = m_ref[...]
    up = mm(right, t22)
    out_ref[:h, :h] = t11 + mm(up, left)
    out_ref[:h, h:] = -up
    out_ref[h:, :h] = -mm(t22, left)
    out_ref[h:, h:] = t22


def inverse(a):
    n = a.shape[0]
    return pl.pallas_call(
        inverse_kernel,
        out_shape=jax.ShapeDtypeStruct(a.shape, jnp.float32),
        scratch_shapes=[
            pltpu.VMEM((n // 2, n // 2), jnp.float32),
            pltpu.VMEM((n // 2, n // 2), jnp.float32),
        ],
        cost_estimate=pl.CostEstimate(
            flops=100_000_000, bytes_accessed=3 * a.size * 4, transcendentals=0
        ),
    )(a)


def per_device(matrix):
    row_count, width = matrix.shape
    rows, xs, zs = lax.axis_size(ROW), lax.axis_size("x"), lax.axis_size("z")
    part = width // rows
    ratio = row_count // width
    row_id = lax.axis_index(ROW)
    col_id = lax.axis_index(COL)
    cols = xs * zs

    def to_block_row(piece):
        pairs = []
        for r in range(rows):
            for c in range(cols):
                pairs.append((r * cols + c, (c // ratio) * cols + (c % ratio) * rows + r))
        return lax.ppermute(piece, EVERY, pairs)

    first = (row_id == 0).astype(jnp.float32)

    panel_c0 = jnp.where(col_id > 0, matrix[:width].T, 0.0)
    piece = exchange(panel_c0.reshape(rows, part, width), ROW)[0]
    along_z = to_all(to_block_row(piece), "z").reshape(zs * part, width)
    panel_r = to_all(along_z, "x").reshape(row_count, width)

    gram_r = tn(panel_r, panel_r)
    top_r = panel_r[width : 2 * width] * first
    both = jnp.concatenate(
        [gram_r.reshape(rows, part, width), top_r.reshape(rows, part, width)], axis=1
    )
    both = jnp.sum(exchange(both, ROW), axis=0)
    three = to_all(jnp.concatenate([both, piece], axis=0), ROW)
    gram = three[:, :part].reshape(width, width)
    top = three[:, part : 2 * part].reshape(width, width)
    panel_c = three[:, 2 * part :].reshape(width, width)

    low = jnp.linalg.cholesky(gram)
    upper = SIGN * low.T
    refl_c = panel_c + jnp.where(col_id == 1, upper, 0.0)
    refl_r = lax.dynamic_update_slice_in_dim(
        panel_r, panel_r[width : 2 * width] + first * upper, width, 0
    )

    x_part = tn(matrix, refl_r)
    y_part = tn(refl_c, x_part)
    both = jnp.concatenate(
        [x_part.reshape(rows, part, width), y_part.reshape(rows, part, width)], axis=1
    )
    both = jnp.sum(exchange(both, ROW), axis=0)
    x_piece, y_piece = both[:part], both[part:]
    x_moved = to_block_row(x_piece)
    tfac = inverse(gram + SIGN * mm(low, top))
    both = to_all(jnp.concatenate([x_moved, y_piece], axis=0), "z")
    x_z = both[:, :part].reshape(zs * part, width)
    y_z = jnp.sum(both[:, part:], axis=0)
    both = to_all(jnp.concatenate([x_z, y_z], axis=0), "x")
    x_r = both[:, : zs * part].reshape(row_count, width)
    y_piece = jnp.sum(both[:, zs * part :], axis=0)
    both = to_all(jnp.concatenate([x_piece, y_piece], axis=0), ROW)
    x_c = both[:, :part].reshape(width, width)
    y_full = both[:, part:].reshape(width, width)

    middle = tn(tfac, mm(y_full, tfac))
    side = mm(x_c, tfac) - mm(refl_c, middle)
    lead = nt(refl_c, tfac)
    return matrix - nt(x_r, lead) - nt(refl_r, side)


def solution(mesh):
    shape = (mesh.shape["row"] // 2, 2, 4, mesh.shape["col"] // 4)
    torus = Mesh(mesh.devices.reshape(shape), EVERY)
    return jax.shard_map(
        per_device,
        mesh=torus,
        in_specs=(P(ROW, COL),),
        out_specs=P(ROW, COL),
        check_vma=False,
    )
```

time: 799 us -> 327 us (0.41)
  waiting for transfers between devices: 516 us -> 43 us
  other arithmetic: 124 us -> 37.1 us
  blocking collectives: 76.6 us -> 156 us
  starting transfers between devices: 0.99 us -> 33.2 us
  Pallas kernels: 0 us -> 31.7 us
  matrix products: 33.2 us -> 13.4 us
  local copies, waits for them, and re-layouts: 27.5 us -> 10.3 us
  between operations: 16.8 us -> 1.61 us
    psum x3 -> x0, waiting for transfers between devices: 349 us -> none  [the longest x2 217 us: spread(): x = lax.psum(x, axis)]
    all_gather x4 -> x0, waiting for transfers between devices: 167 us -> none  [the longest x2 107 us: from_root(): lax.all_gather(x, axis)]
    all_to_all x1 -> x6, blocking collectives: 66.6 us -> 156 us  [exchange(): return lax.all_to_all(tiles, axis, 0, 0, tiled=True)]
    another operation x18 -> x6, other arithmetic: 113 us -> 34 us  [per_device(): low = jnp.linalg.cholesky(gram)]
    pallas_call x0 -> x1, Pallas kernels: none -> 31.7 us  [inverse(): pl.pallas_call(inverse_kernel, out_shape=jax.ShapeDtypeStruct(a.shape, jn...]
    all_to_all x0 -> x3, waiting for transfers between devices: none -> 31.6 us  [exchange(): return lax.all_to_all(tiles, axis, 0, 0, tiled=True)]
    all_to_all x0 -> x3, starting transfers between devices: none -> 26.6 us  [exchange(): return lax.all_to_all(tiles, axis, 0, 0, tiled=True)]
    another operation x16 -> x2, matrix products: 15.1 us -> 0.47 us  [per_device(): low = jnp.linalg.cholesky(gram)]
  transfers between devices with their start and end apart: 7 -> 5, of which waited for: 6 -> 4; matrix products, arithmetic and copies ran while one was open for 11% -> 2% of each run, Pallas kernels for 0% -> 10%
where the time goes in v1:
time: 327 us; the launch traced here: 326 us
  blocking collectives  156 us (48%)
  waiting for transfers between devices  43 us (13%)
  other arithmetic  37.1 us (11%)
  starting transfers between devices  33.2 us (10%)
  Pallas kernels  31.7 us (10%)
  matrix products  13.4 us (4%)
  local copies, waits for them, and re-layouts  10.3 us (3%)
    all_to_all x6, blocking collectives, exchange(): return lax.all_to_all(tiles, axis, 0, 0, tiled=True)  156 us
    another operation x6, other arithmetic, per_device(): low = jnp.linalg.cholesky(gram)  34 us
    pallas_call x1, Pallas kernels, inverse(): pl.pallas_call(inverse_kernel, out_shape=jax.ShapeDtypeStruct(a.shape, jn...  31.7 us
    all_to_all x3, waiting for transfers between devices, exchange(): return lax.all_to_all(tiles, axis, 0, 0, tiled=True)  31.6 us
    all_to_all x3, starting transfers between devices, exchange(): return lax.all_to_all(tiles, axis, 0, 0, tiled=True)  26.6 us
    dot_general x11, matrix products, dot(): lax.dot_general(left, right, (dims, ((), ())), precision=lax.Precision.HI...  13 us
    ppermute x2, waiting for transfers between devices, to_block_row(): return lax.ppermute(piece, EVERY, pairs)  11.4 us
    ppermute x2, starting transfers between devices, to_block_row(): return lax.ppermute(piece, EVERY, pairs)  6.62 us
  transfers between devices with their start and end apart: 5, of which 4 were waited for; matrix products, arithmetic and copies ran while one was open for 2% of the time, Pallas kernels for 10%

profile of v1, /device:TPU:1, one launch (start us, length us, event | category | flops | bytes accessed | tf_op | source)
XLA Modules:
  0.0 326.5 jit_solution(4590082911803843762)
XLA Ops:
  1.1 28.3 %all_to_all.45 = f32[16,16,256]{2,1,0:T(8,128)S(1)} all-to-all(f32[16,16,256]{2,1,0:T(8,128)S(1)} %bitcast.76), channel_id=1, replica_groups=mesh['y'=8,'core'=2,'x'=4,'z'=16] {'y','core'}, dimensions={0} | all-to-all | bytes 524288 | tf_op jit(solution)/shard_map/all_to_all | solution.py:38
  29.4 1.9 collective-permute-start
  31.3 7.1 %collective-permute-done = f32[16,256]{1,0:T(8,128)S(1)} collective-permute-done((f32[16,256]{1,0:T(8,128)S(1)}, f32[16,256]{1,0:T(8,128)S(1)}, u32[]{:S(2)}, u32[]{:S(2)}) %collective-permute-start) | collective-permute-done | bytes 16416 | tf_op jit(solution)/shard_map/ppermute | solution.py:114
  38.5 29.3 %all_to_all.46 = f32[16,16,256]{2,1,0:T(8,128)S(1)} all-to-all(f32[16,16,256]{2,1,0:T(8,128)S(1)} %broadcast_in_dim.22), channel_id=1, replica_groups=mesh['y'=8,'core'=2,'x'=4,'z'=16] {'z'}, dimensions={0} | all-to-all | bytes 524288 | tf_op jit(solution)/shard_map/all_to_all | solution.py:38
  69.0 5.5 %all-to-all-start.2 = ((f32[4,256,256]{1,2,0:T(8,128)}), f32[4,256,256]{1,2,0:T(8,128)S(1)}, u32[]{:S(2)}, u32[]{:S(2)}) async-start(f32[4,256,256]{1,2,0:T(8,128)} %broadcast_in_dim.24), calls=%async_computation.2 | async-start | bytes 2097152 | tf_op jit(solution)/shard_map/all_to_all | solution.py:38
  74.5 9.7 %all-to-all-done.2 = f32[4,256,256]{1,2,0:T(8,128)S(1)} async-done(((f32[4,256,256]{1,2,0:T(8,128)}), f32[4,256,256]{1,2,0:T(8,128)S(1)}, u32[]{:S(2)}, u32[]{:S(2)}) %all-to-all-start.2) | async-done | bytes 1048608 | tf_op jit(solution)/shard_map/all_to_all | solution.py:38
  86.2 28.5 %all_to_all.47 = f32[16,32,256]{2,1,0:T(8,128)S(1)} all-to-all(f32[16,32,256]{2,1,0:T(8,128)S(1)} %pad_maximum_fusion), channel_id=1, replica_groups=mesh['y'=8,'core'=2,'x'=4,'z'=16] {'y','core'}, dimensions={0} | all-to-all | bytes 1048576 | tf_op jit(solution)/shard_map/all_to_all | solution.py:38
  115.7 3.7 %all-to-all-start.4 = ((f32[16,48,256]{2,1,0:T(8,128)}), f32[16,48,256]{2,1,0:T(8,128)S(1)}, u32[]{:S(2)}, u32[]{:S(2)}) async-start(f32[16,48,256]{2,1,0:T(8,128)} %broadcast_in_dim.25), calls=%async_computation.4 | async-start | bytes 1572864 | tf_op jit(solution)/shard_map/all_to_all | solution.py:38
  119.4 21.9 %all-to-all-done.4 = f32[16,48,256]{2,1,0:T(8,128)S(1)} async-done(((f32[16,48,256]{2,1,0:T(8,128)}), f32[16,48,256]{2,1,0:T(8,128)S(1)}, u32[]{:S(2)}, u32[]{:S(2)}) %all-to-all-start.4) | async-done | bytes 786464 | tf_op jit(solution)/shard_map/all_to_all | solution.py:38
  142.2 11.7 %cholesky.49 = f32[128,128]{1,0:T(8,128)S(1)} custom-call(f32[128,128]{1,0:T(8,128)S(1)} %cholesky.115), custom_call_target="Cholesky" | custom-call | tf_op jit(solution)/shard_map/jit(cholesky)/cholesky | solution.py:134
  154.8 9.8 %custom-call.11 = f32[1,128,128]{1,2,0:T(8,128)S(1)} custom-call(f32[1,128,128]{2,1,0:T(8,128)S(1)} %get-tuple-element.17), custom_call_target="InvertDiagBlocksLowerTriangular" | custom-call | tf_op jit(solution)/shard_map/jit(cholesky)/cholesky | solution.py:134
  165.1 11.7 %cholesky.103 = f32[128,128]{1,0:T(8,128)S(1)} custom-call(f32[128,128]{1,0:T(8,128)S(1)} %convolution_subtract_fusion.3), custom_call_target="Cholesky" | custom-call | tf_op jit(solution)/shard_map/jit(cholesky)/cholesky | solution.py:134
  178.9 1.9 bitcast_add_fusion.1
  181.9 2.0 fusion.14
  184.3 20.1 %all_to_all.48 = f32[16,32,256]{2,1,0:T(8,128)S(1)} all-to-all(f32[16,32,256]{2,1,0:T(8,128)S(1)} %pad_maximum_fusion.1), channel_id=1, replica_groups=mesh['y'=8,'core'=2,'x'=4,'z'=16] {'y','core'}, dimensions={0} | all-to-all | bytes 1048576 | tf_op jit(solution)/shard_map/all_to_all | solution.py:38
  204.5 4.7 %collective-permute-start.1 = (f32[16,256]{1,0:T(8,128)S(1)}, f32[16,256]{1,0:T(8,128)S(1)}, u32[]{:S(2)}, u32[]{:S(2)}) collective-permute-start(f32[16,256]{1,0:T(8,128)S(1)} %get-tuple-element.18), channel_id=1, source_target_pairs={{0,0},{1,16},{2,32},{3,48},{4,64},{5,80},{6,96},{7,112},{8,128},{9... | collective-permute-start | bytes 49160 | tf_op jit(solution)/shard_map/ppermute | solution.py:114
  209.3 4.2 %collective-permute-done.1 = f32[16,256]{1,0:T(8,128)S(1)} collective-permute-done((f32[16,256]{1,0:T(8,128)S(1)}, f32[16,256]{1,0:T(8,128)S(1)}, u32[]{:S(2)}, u32[]{:S(2)}) %collective-permute-start.1) | collective-permute-done | bytes 16416 | tf_op jit(solution)/shard_map/ppermute | solution.py:114
  213.6 36.8 %all_to_all.49 = f32[16,32,256]{2,1,0:T(8,128)S(1)} all-to-all(f32[16,32,256]{2,1,0:T(8,128)S(1)} %broadcast_in_dim.26), channel_id=1, replica_groups=mesh['y'=8,'core'=2,'x'=4,'z'=16] {'z'}, dimensions={0} | all-to-all | bytes 1048576 | tf_op jit(solution)/shard_map/all_to_all | solution.py:38
  250.5 13.1 %all_to_all.50 = f32[4,272,256]{2,1,0:T(8,128)S(1)} all-to-all(f32[4,272,256]{2,1,0:T(8,128)S(1)} %broadcast_in_dim.50), channel_id=1, replica_groups=mesh['y'=8,'core'=2,'x'=4,'z'=16] {'x'}, dimensions={0} | all-to-all | bytes 2228224 | tf_op jit(solution)/shard_map/all_to_all | solution.py:38
  265.5 17.3 %all-to-all-start.8 = ((f32[16,32,256]{2,1,0:T(8,128)}), f32[16,32,256]{2,1,0:T(8,128)S(1)}, u32[]{:S(2)}, u32[]{:S(2)}) async-start(f32[16,32,256]{2,1,0:T(8,128)} %broadcast_in_dim.51), calls=%async_computation.8 | async-start | bytes 1048576 | tf_op jit(solution)/shard_map/all_to_all | solution.py:38
  282.9 2.0 convolution_add_fusion.a_ref
  284.9 31.7 %shard_map.17 = f32[256,256]{1,0:T(8,128)} custom-call(f32[256,256]{1,0:T(8,128)} %convolution_add_fusion.a_ref), custom_call_target="tpu_custom_call" | custom-call | flops 100000000 | bytes 786432 | tf_op jit(solution)/shard_map/pallas_call | solution.py:87
  319.3 2.0 convolution_subtract_fusion.1
  324.5 2.0 convolution_subtract_fusion
  (65 shorter events, 17.7 us)
Async XLA Ops:
  29.4 9.1 %collective-permute-start = (f32[16,256]{1,0:T(8,128)S(1)}, f32[16,256]{1,0:T(8,128)S(1)}, u32[]{:S(2)}, u32[]{:S(2)}) collective-permute-start(f32[16,256]{1,0:T(8,128)S(1)} %slice_bitcast_fusion), channel_id=1, source_target_pairs={{0,0},{1,16},{2,32},{3,48},{4,64},{5,80},{6,96},{7,112},{8,128},{9... | collective-permute-start | bytes 49160 | tf_op jit(solution)/shard_map/ppermute | solution.py:114
  69.0 15.3 %all-to-all-start.2 = ((f32[4,256,256]{1,2,0:T(8,128)}), f32[4,256,256]{1,2,0:T(8,128)S(1)}, u32[]{:S(2)}, u32[]{:S(2)}) async-start(f32[4,256,256]{1,2,0:T(8,128)} %broadcast_in_dim.24), calls=%async_computation.2 | async-start | bytes 2097152 | tf_op jit(solution)/shard_map/all_to_all | solution.py:38
  115.7 25.6 %all-to-all-start.4 = ((f32[16,48,256]{2,1,0:T(8,128)}), f32[16,48,256]{2,1,0:T(8,128)S(1)}, u32[]{:S(2)}, u32[]{:S(2)}) async-start(f32[16,48,256]{2,1,0:T(8,128)} %broadcast_in_dim.25), calls=%async_computation.4 | async-start | bytes 1572864 | tf_op jit(solution)/shard_map/all_to_all | solution.py:38
  142.0 12.8 %copy-start.4 = (f32[16,16,256]{2,1,0:T(8,128)}, f32[16,16,256]{2,1,0:T(8,128)S(1)}, u32[]{:S(2)}) copy-start(f32[16,16,256]{2,1,0:T(8,128)S(1)} %get-tuple-element.7) | copy-start | bytes 786436
  176.9 2.0 copy-start.6
  178.9 3.0 copy-start.1
  204.5 9.0 %collective-permute-start.1 = (f32[16,256]{1,0:T(8,128)S(1)}, f32[16,256]{1,0:T(8,128)S(1)}, u32[]{:S(2)}, u32[]{:S(2)}) collective-permute-start(f32[16,256]{1,0:T(8,128)S(1)} %get-tuple-element.18), channel_id=1, source_target_pairs={{0,0},{1,16},{2,32},{3,48},{4,64},{5,80},{6,96},{7,112},{8,128},{9... | collective-permute-start | bytes 49160 | tf_op jit(solution)/shard_map/ppermute | solution.py:114
  263.6 1.0 copy-start.2
  264.6 18.2 %copy-start.5 = (f32[16,16,256]{2,1,0:T(8,128)S(1)}, f32[16,16,256]{2,1,0:T(8,128)}, u32[]{:S(2)}) copy-start(f32[16,16,256]{2,1,0:T(8,128)} %copy-done.4) | copy-start | bytes 786436
  264.6 18.2 %copy-start.7 = (f32[256,256]{1,0:T(8,128)S(1)}, f32[256,256]{1,0:T(8,128)}, u32[]{:S(2)}) copy-start(f32[256,256]{1,0:T(8,128)} %copy-done.6) | copy-start | bytes 786436
  265.5 55.8 %all-to-all-start.8 = ((f32[16,32,256]{2,1,0:T(8,128)}), f32[16,32,256]{2,1,0:T(8,128)S(1)}, u32[]{:S(2)}, u32[]{:S(2)}) async-start(f32[16,32,256]{2,1,0:T(8,128)} %broadcast_in_dim.51), calls=%async_computation.8 | async-start | bytes 1048576 | tf_op jit(solution)/shard_map/all_to_all | solution.py:38
  318.1 1.2 slice-start
  321.3 0.9 copy-start
  323.3 1.2 copy-start.3

commit v2 on v1

v2 whole, which is shorter than its diff:
```python
import jax
import jax.numpy as jnp
from jax import lax
from jax.experimental import pallas as pl
from jax.experimental.pallas import tpu as pltpu
from jax.sharding import Mesh
from jax.sharding import PartitionSpec as P

ROW = ("y", "core")
COL = ("x", "z")
EVERY = ROW + COL
SIGN = 1.0


def dot(left, right, dims, precision):
    return lax.dot_general(
        left,
        right,
        (dims, ((), ())),
        precision=precision,
        preferred_element_type=jnp.float32,
    )


def mm(left, right, precision=lax.Precision.HIGHEST):
    return dot(left, right, ((1,), (0,)), precision)


def tn(left, right, precision=lax.Precision.HIGHEST):
    return dot(left, right, ((0,), (0,)), precision)


def nt(left, right, precision=lax.Precision.HIGHEST):
    return dot(left, right, ((1,), (1,)), precision)


def exchange(tiles, axis):
    return lax.all_to_all(tiles, axis, 0, 0, tiled=True)


def to_all(piece, axis):
    n = lax.axis_size(axis)
    return exchange(jnp.broadcast_to(piece[None], (n, *piece.shape)), axis)


def invert_half(m_ref, c_ref):
    n = m_ref.shape[0]
    lanes = lax.broadcasted_iota(jnp.int32, (n, n), 1)
    subs = lax.broadcasted_iota(jnp.int32, (n, n), 0)
    lane_row = lax.broadcasted_iota(jnp.int32, (1, n), 1)

    def step(k, carry):
        m = m_ref[...]
        hit = lanes == k
        col = jnp.sum(jnp.where(hit, m, 0.0), axis=1, keepdims=True)
        c_ref[...] = jnp.broadcast_to(col, (n, n))
        pivot = c_ref[pl.ds(k, 1), :]
        row = jnp.where(lane_row == k, 1.0, m_ref[pl.ds(k, 1), :]) / pivot
        rest = jnp.where(hit, 0.0, m) - c_ref[...] * row
        m_ref[...] = jnp.where(subs == k, row, rest)
        return carry

    lax.fori_loop(0, n, step, 0)


def first_half(a_ref, t11_ref, right_ref, left_ref, schur_ref, m_ref, c_ref):
    h = a_ref.shape[0] // 2
    m_ref[...] = a_ref[:h, :h]
    invert_half(m_ref, c_ref)
    t11 = m_ref[...]
    right = mm(t11, a_ref[:h, h:])
    t11_ref[...] = t11
    right_ref[...] = right
    left_ref[...] = mm(a_ref[h:, :h], t11)
    schur_ref[...] = a_ref[h:, h:] - mm(a_ref[h:, :h], right)


def second_half(t11_ref, right_ref, left_ref, schur_ref, out_ref, m_ref, c_ref):
    h = t11_ref.shape[0]
    m_ref[...] = schur_ref[...]
    invert_half(m_ref, c_ref)
    t22 = m_ref[...]
    up = mm(right_ref[...], t22)
    out_ref[:h, :h] = t11_ref[...] + mm(up, left_ref[...])
    out_ref[:h, h:] = -up
    out_ref[h:, :h] = -mm(t22, left_ref[...])
    out_ref[h:, h:] = t22


COST = pl.CostEstimate(flops=2_000_000_000, bytes_accessed=500_000, transcendentals=0)


def half_inverted(a):
    half = jax.ShapeDtypeStruct((a.shape[0] // 2, a.shape[1] // 2), jnp.float32)
    return pl.pallas_call(
        first_half,
        out_shape=[half] * 4,
        scratch_shapes=[pltpu.VMEM(half.shape, jnp.float32)] * 2,
        cost_estimate=COST,
    )(a)


def inverted(parts):
    h = parts[0].shape[0]
    return pl.pallas_call(
        second_half,
        out_shape=jax.ShapeDtypeStruct((2 * h, 2 * h), jnp.float32),
        scratch_shapes=[pltpu.VMEM((h, h), jnp.float32)] * 2,
        cost_estimate=COST,
    )(*parts)


def per_device(matrix):
    row_count, width = matrix.shape
    rows, xs, zs = lax.axis_size(ROW), lax.axis_size("x"), lax.axis_size("z")
    part = width // rows
    ratio = row_count // width
    row_id = lax.axis_index(ROW)
    col_id = lax.axis_index(COL)
    cols = xs * zs

    def to_block_row(piece):
        pairs = []
        for r in range(rows):
            for c in range(cols):
                pairs.append((r * cols + c, (c // ratio) * cols + (c % ratio) * rows + r))
        return lax.ppermute(piece, EVERY, pairs)

    first = (row_id == 0).astype(jnp.float32)
    fast = lax.Precision.HIGH

    panel_c0 = jnp.where(col_id > 0, matrix[:width].T, 0.0)
    head, below = matrix[:width], matrix[width:]
    gram_r = tn(below, below) + tn(head * (1.0 - first), head)
    both = exchange(
        jnp.concatenate(
            [panel_c0.reshape(rows, part, width), gram_r.reshape(rows, part, width)], axis=1
        ),
        ROW,
    )
    piece = both[0, :part]
    gram_piece = jnp.sum(both[:, part:], axis=0)
    moved = to_block_row(piece)

    lead = to_all(jnp.where(col_id == 0, gram_piece, piece), "x")[0]
    lead = to_all(lead, "z")[:2].reshape(2 * part, width)
    lead = to_all(jnp.concatenate([lead, piece], axis=0), ROW)
    lead, moved = lax.optimization_barrier((lead, moved))
    gram = lead[:, :part].reshape(width, width)
    top = lead[:, part : 2 * part].reshape(width, width)
    panel_c = lead[:, 2 * part :].reshape(width, width)

    along_z = to_all(moved, "z").reshape(zs * part, width)
    panel_r = to_all(along_z, "x").reshape(row_count, width)
    low = lax.linalg.cholesky(gram, symmetrize_input=False)
    upper = SIGN * low.T
    parts = half_inverted(gram + SIGN * mm(low, top))
    refl_c = panel_c + jnp.where(col_id == 1, upper, 0.0)
    refl_r = lax.dynamic_update_slice_in_dim(
        panel_r, panel_r[width : 2 * width] + first * upper, width, 0
    )

    x_part = tn(matrix, refl_r, fast)
    y_part = tn(refl_c, x_part)
    both = jnp.concatenate(
        [x_part.reshape(rows, part, width), y_part.reshape(rows, part, width)], axis=1
    )
    both = jnp.sum(exchange(both, ROW), axis=0)
    x_piece, y_piece = both[:part], both[part:]
    x_moved = to_block_row(x_piece)
    y_z = to_all(y_piece, "z")
    x_moved, y_z = lax.optimization_barrier((x_moved, y_z))
    y_z = jnp.sum(y_z, axis=0)
    x_z = to_all(x_moved, "z").reshape(zs * part, width)
    both, parts = lax.optimization_barrier((jnp.concatenate([x_z, y_z], axis=0), parts))
    both = to_all(both, "x")
    tfac = inverted(parts)
    x_r = both[:, : zs * part].reshape(row_count, width)
    y_piece = jnp.sum(both[:, zs * part :], axis=0)
    both = jnp.concatenate([x_piece, y_piece], axis=0)
    both, tfac = lax.optimization_barrier((both, tfac))
    both = to_all(both, ROW)
    x_c = both[:, :part].reshape(width, width)
    y_full = both[:, part:].reshape(width, width)

    middle = tn(tfac, mm(y_full, tfac))
    side = mm(x_c, tfac) - mm(refl_c, middle)
    lead = nt(refl_c, tfac)
    return matrix - nt(x_r, lead, fast) - nt(refl_r, side, fast)


def solution(mesh):
    shape = (mesh.shape["row"] // 2, 2, 4, mesh.shape["col"] // 4)
    torus = Mesh(mesh.devices.reshape(shape), EVERY)
    return jax.shard_map(
        per_device,
        mesh=torus,
        in_specs=(P(ROW, COL),),
        out_specs=P(ROW, COL),
        check_vma=False,
    )
```

time: 327 us -> 291 us (0.89)
  blocking collectives: 156 us -> 53.3 us
  starting transfers between devices: 33.2 us -> 74.5 us
  waiting for transfers between devices: 43 us -> 69.4 us
    all_to_all x6 -> x3, blocking collectives: 156 us -> 53.3 us  [exchange(): return lax.all_to_all(tiles, axis, 0, 0, tiled=True)]
    all_to_all x3 -> x8, starting transfers between devices: 26.6 us -> 68.5 us  [exchange(): return lax.all_to_all(tiles, axis, 0, 0, tiled=True)]
    all_to_all x3 -> x8, waiting for transfers between devices: 31.6 us -> 51 us  [exchange(): return lax.all_to_all(tiles, axis, 0, 0, tiled=True)]
    ppermute x2, waiting for transfers between devices: 11.4 us -> 18.3 us  [to_block_row(): return lax.ppermute(piece, EVERY, pairs)]
    dot_general x11 -> x12, matrix products: 13 us -> 10.8 us  [dot(): lax.dot_general(left, right, (dims, ((), ())), precision=precision, prefe...]
    pallas_call x1 -> x2, Pallas kernels: 31.7 us -> 32.9 us  [the longest x1 16.5 us: inverted(): pl.pallas_call(second_half, out_shape=jax.ShapeDtypeStruct((2 * h, 2 * h)...]
  transfers between devices with their start and end apart: 5 -> 10, of which waited for: 4 -> 7; matrix products, arithmetic and copies ran while one was open for 2% -> 13% of each run, Pallas kernels for 10% -> 11%
where the time goes in v2:
time: 291 us; the launch traced here: 290 us
  starting transfers between devices  74.5 us (26%)
  waiting for transfers between devices  69.4 us (24%)
  blocking collectives  53.3 us (18%)
  other arithmetic  35.1 us (12%)
  Pallas kernels  32.9 us (11%)
  local copies, waits for them, and re-layouts  11.6 us (4%)
  matrix products  11.3 us (4%)
    all_to_all x8, starting transfers between devices, exchange(): return lax.all_to_all(tiles, axis, 0, 0, tiled=True)  68.5 us
    all_to_all x3, blocking collectives, exchange(): return lax.all_to_all(tiles, axis, 0, 0, tiled=True)  53.3 us
    all_to_all x8, waiting for transfers between devices, exchange(): return lax.all_to_all(tiles, axis, 0, 0, tiled=True)  51 us
    another operation x6, other arithmetic, per_device(): low = lax.linalg.cholesky(gram, symmetrize_input=False)  34 us
    ppermute x2, waiting for transfers between devices, to_block_row(): return lax.ppermute(piece, EVERY, pairs)  18.3 us
    pallas_call x1, Pallas kernels, inverted(): pl.pallas_call(second_half, out_shape=jax.ShapeDtypeStruct((2 * h, 2 * h)...  16.5 us
    pallas_call x1, Pallas kernels, half_inverted(): pl.pallas_call(first_half, out_shape=[half] * 4, scratch_shapes=[pltpu.VM...  16.4 us
    dot_general x12, matrix products, dot(): lax.dot_general(left, right, (dims, ((), ())), precision=precision, prefe...  10.8 us
  transfers between devices with their start and end apart: 10, of which 7 were waited for; matrix products, arithmetic and copies ran while one was open for 13% of the time, Pallas kernels for 11%

profile of v2, /device:TPU:1, one launch (start us, length us, event | category | flops | bytes accessed | tf_op | source)
XLA Modules:
  0.0 289.8 jit_solution(17006016363945430068)
XLA Ops:
  0.0 3.0 %fusion = f32[256,256]{1,0:T(8,128)S(1)} fusion(f32[1024,256]{1,0:T(8,128)} %param.1), kind=kOutput, calls=%fused_computation.6 | convolution fusion | flops 603979776 | bytes 1048576 | tf_op jit(solution)/shard_map/dot_general | solution.py:16
  4.6 17.5 %all-to-all-start = ((f32[16,32,256]{2,1,0:T(8,128)}), f32[16,32,256]{2,1,0:T(8,128)S(1)}, u32[]{:S(2)}, u32[]{:S(2)}) async-start(f32[16,32,256]{2,1,0:T(8,128)} %pad_maximum_fusion), calls=%async_computation | async-start | bytes 1048576 | tf_op jit(solution)/shard_map/all_to_all | solution.py:38
  22.1 17.3 %all-to-all-done = f32[16,32,256]{2,1,0:T(8,128)S(1)} async-done(((f32[16,32,256]{2,1,0:T(8,128)}), f32[16,32,256]{2,1,0:T(8,128)S(1)}, u32[]{:S(2)}, u32[]{:S(2)}) %all-to-all-start) | async-done | bytes 524320 | tf_op jit(solution)/shard_map/all_to_all | solution.py:38
  39.5 6.8 %all_to_all.55 = f32[4,16,256]{2,1,0:T(8,128)S(1)} all-to-all(f32[4,16,256]{2,1,0:T(8,128)S(1)} %broadcast_in_dim.31), channel_id=1, replica_groups=mesh['y'=8,'core'=2,'x'=4,'z'=16] {'x'}, dimensions={0} | all-to-all | bytes 131072 | tf_op jit(solution)/shard_map/all_to_all | solution.py:38
  46.3 24.9 %all_to_all.56 = f32[16,16,256]{2,1,0:T(8,128)S(1)} all-to-all(f32[16,16,256]{2,1,0:T(8,128)S(1)} %broadcast_in_dim.33), channel_id=1, replica_groups=mesh['y'=8,'core'=2,'x'=4,'z'=16] {'z'}, dimensions={0} | all-to-all | bytes 524288 | tf_op jit(solution)/shard_map/all_to_all | solution.py:38
  72.2 8.5 %all-to-all-start.3 = ((f32[16,48,256]{2,1,0:T(8,128)}), f32[16,48,256]{2,1,0:T(8,128)S(1)}, u32[]{:S(2)}, u32[]{:S(2)}) async-start(f32[16,48,256]{2,1,0:T(8,128)} %broadcast_in_dim.34), calls=%async_computation.3 | async-start | bytes 1572864 | tf_op jit(solution)/shard_map/all_to_all | solution.py:38
  80.7 3.5 %collective-permute-start = (f32[16,256]{1,0:T(8,128)S(1)}, f32[16,256]{1,0:T(8,128)S(1)}, u32[]{:S(2)}, u32[]{:S(2)}) collective-permute-start(f32[16,256]{1,0:T(8,128)S(1)} %get-tuple-element.41), channel_id=1, source_target_pairs={{0,0},{1,16},{2,32},{3,48},{4,64},{5,80},{6,96},{7,112},{8,128},{9... | collective-permute-start | bytes 49160 | tf_op jit(solution)/shard_map/ppermute | solution.py:127
  84.3 5.4 %collective-permute-done = f32[16,256]{1,0:T(8,128)S(1)} collective-permute-done((f32[16,256]{1,0:T(8,128)S(1)}, f32[16,256]{1,0:T(8,128)S(1)}, u32[]{:S(2)}, u32[]{:S(2)}) %collective-permute-start) | collective-permute-done | bytes 16416 | tf_op jit(solution)/shard_map/ppermute | solution.py:127
  89.7 13.8 %all-to-all-done.3 = f32[16,48,256]{2,1,0:T(8,128)S(1)} async-done(((f32[16,48,256]{2,1,0:T(8,128)}), f32[16,48,256]{2,1,0:T(8,128)S(1)}, u32[]{:S(2)}, u32[]{:S(2)}) %all-to-all-start.3) | async-done | bytes 786464 | tf_op jit(solution)/shard_map/all_to_all | solution.py:38
  104.2 7.1 %all-to-all-start.4 = ((f32[16,16,256]{2,1,0:T(8,128)}), f32[16,16,256]{2,1,0:T(8,128)S(1)}, u32[]{:S(2)}, u32[]{:S(2)}) async-start(f32[16,16,256]{2,1,0:T(8,128)} %broadcast_in_dim.35), calls=%async_computation.4 | async-start | bytes 524288 | tf_op jit(solution)/shard_map/all_to_all | solution.py:38
  112.1 11.7 %cholesky.49 = f32[128,128]{1,0:T(8,128)S(1)} custom-call(f32[128,128]{1,0:T(8,128)S(1)} %cholesky.115), custom_call_target="Cholesky" | custom-call | tf_op jit(solution)/shard_map/cholesky | solution.py:155
  123.8 9.8 %custom-call.8 = f32[1,128,128]{1,2,0:T(8,128)S(1)} custom-call(f32[1,128,128]{2,1,0:T(8,128)S(1)} %get-tuple-element.47), custom_call_target="InvertDiagBlocksLowerTriangular" | custom-call | tf_op jit(solution)/shard_map/cholesky | solution.py:155
  134.9 3.7 %all-to-all-start.5 = ((f32[4,256,256]{1,2,0:T(8,128)}), f32[4,256,256]{1,2,0:T(8,128)S(1)}, u32[]{:S(2)}, u32[]{:S(2)}) async-start(f32[4,256,256]{1,2,0:T(8,128)} %broadcast_in_dim.72), calls=%async_computation.5 | async-start | bytes 2097152 | tf_op jit(solution)/shard_map/all_to_all | solution.py:38
  139.1 11.7 %cholesky.103 = f32[128,128]{1,0:T(8,128)S(1)} custom-call(f32[128,128]{1,0:T(8,128)S(1)} %convolution_subtract_fusion.3), custom_call_target="Cholesky" | custom-call | tf_op jit(solution)/shard_map/cholesky | solution.py:155
  157.6 21.5 %all_to_all.57 = f32[16,32,256]{2,1,0:T(8,128)S(1)} all-to-all(f32[16,32,256]{2,1,0:T(8,128)S(1)} %pad_maximum_fusion.1), channel_id=1, replica_groups=mesh['y'=8,'core'=2,'x'=4,'z'=16] {'y','core'}, dimensions={0} | all-to-all | bytes 1048576 | tf_op jit(solution)/shard_map/all_to_all | solution.py:38
  179.9 11.7 %all-to-all-start.7 = ((f32[16,16,256]{2,1,0:T(8,128)}), f32[16,16,256]{2,1,0:T(8,128)S(1)}, u32[]{:S(2)}, u32[]{:S(2)}) async-start(f32[16,16,256]{2,1,0:T(8,128)} %broadcast_in_dim.73), calls=%async_computation.7 | async-start | bytes 524288 | tf_op jit(solution)/shard_map/all_to_all | solution.py:38
  194.2 12.9 %collective-permute-done.1 = f32[16,256]{1,0:T(8,128)S(1)} collective-permute-done((f32[16,256]{1,0:T(8,128)S(1)}, f32[16,256]{1,0:T(8,128)S(1)}, u32[]{:S(2)}, u32[]{:S(2)}) %collective-permute-start.1) | collective-permute-done | bytes 16416 | tf_op jit(solution)/shard_map/ppermute | solution.py:127
  207.1 4.1 %all-to-all-done.7 = f32[16,16,256]{2,1,0:T(8,128)S(1)} async-done(((f32[16,16,256]{2,1,0:T(8,128)}), f32[16,16,256]{2,1,0:T(8,128)S(1)}, u32[]{:S(2)}, u32[]{:S(2)}) %all-to-all-start.7) | async-done | bytes 262176 | tf_op jit(solution)/shard_map/all_to_all | solution.py:38
  211.9 5.7 %all-to-all-start.8 = ((f32[16,16,256]{2,1,0:T(8,128)}), f32[16,16,256]{2,1,0:T(8,128)S(1)}, u32[]{:S(2)}, u32[]{:S(2)}) async-start(f32[16,16,256]{2,1,0:T(8,128)} %broadcast_in_dim.74), calls=%async_computation.8 | async-start | bytes 524288 | tf_op jit(solution)/shard_map/all_to_all | solution.py:38
  218.8 16.4 %shard_map.17 = (f32[128,128]{1,0:T(8,128)}, f32[128,128]{1,0:T(8,128)}, f32[128,128]{1,0:T(8,128)}, f32[128,128]{1,0:T(8,128)}) custom-call(f32[256,256]{1,0:T(8,128)} %convolution_add_fusion.a_ref), custom_call_target="tpu_custom_call" | custom-call | flops 2000000000 | bytes 500000 | tf_op jit(solution)/shard_map/pallas_call | solution.py:95
  236.3 4.9 %all-to-all-start.9 = ((f32[4,272,256]{2,1,0:T(8,128)}), f32[4,272,256]{2,1,0:T(8,128)S(1)}, u32[]{:S(2)}, u32[]{:S(2)}) async-start(f32[4,272,256]{2,1,0:T(8,128)} %broadcast_in_dim.75), calls=%async_computation.9 | async-start | bytes 2228224 | tf_op jit(solution)/shard_map/all_to_all | solution.py:38
  241.2 16.5 %shard_map.18 = f32[256,256]{1,0:T(8,128)} custom-call(f32[128,128]{1,0:T(8,128)} %get-tuple-element.29.t11_ref, f32[128,128]{1,0:T(8,128)} %get-tuple-element.30.right_ref, f32[128,128]{1,0:T(8,128)} %get-tuple-element.31.left_ref, f32[128,128]{1,0:T(8,128)} %get-tuple-element.32.schur_ref), custom_call_target="tpu_custom_call" | custom-call | flops 2000000000 | bytes 500000 | tf_op jit(solution)/shard_map/pallas_call | solution.py:105
  258.6 9.3 %all-to-all-start.10 = ((f32[16,32,256]{2,1,0:T(8,128)}), f32[16,32,256]{2,1,0:T(8,128)}, u32[]{:S(2)}, u32[]{:S(2)}) async-start(f32[16,32,256]{2,1,0:T(8,128)} %broadcast_in_dim.76), calls=%async_computation.10 | async-start | bytes 1048576 | tf_op jit(solution)/shard_map/all_to_all | solution.py:38
  270.1 15.0 %all-to-all-done.10 = f32[16,32,256]{2,1,0:T(8,128)} async-done(((f32[16,32,256]{2,1,0:T(8,128)}), f32[16,32,256]{2,1,0:T(8,128)}, u32[]{:S(2)}, u32[]{:S(2)}) %all-to-all-start.10) | async-done | bytes 524320 | tf_op jit(solution)/shard_map/all_to_all | solution.py:38
  (76 shorter events, 25.1 us)
Async XLA Ops:
  0.0 3.0 %copy-start = (f32[1024,256]{1,0:T(8,128)S(1)}, f32[1024,256]{1,0:T(8,128)}, u32[]{:S(2)}) copy-start(f32[1024,256]{1,0:T(8,128)} %param.1) | copy-start | bytes 3145732
  4.6 34.8 %all-to-all-start = ((f32[16,32,256]{2,1,0:T(8,128)}), f32[16,32,256]{2,1,0:T(8,128)S(1)}, u32[]{:S(2)}, u32[]{:S(2)}) async-start(f32[16,32,256]{2,1,0:T(8,128)} %pad_maximum_fusion), calls=%async_computation | async-start | bytes 1048576 | tf_op jit(solution)/shard_map/all_to_all | solution.py:38
  72.2 31.3 %all-to-all-start.3 = ((f32[16,48,256]{2,1,0:T(8,128)}), f32[16,48,256]{2,1,0:T(8,128)S(1)}, u32[]{:S(2)}, u32[]{:S(2)}) async-start(f32[16,48,256]{2,1,0:T(8,128)} %broadcast_in_dim.34), calls=%async_computation.3 | async-start | bytes 1572864 | tf_op jit(solution)/shard_map/all_to_all | solution.py:38
  80.7 9.0 %collective-permute-start = (f32[16,256]{1,0:T(8,128)S(1)}, f32[16,256]{1,0:T(8,128)S(1)}, u32[]{:S(2)}, u32[]{:S(2)}) collective-permute-start(f32[16,256]{1,0:T(8,128)S(1)} %get-tuple-element.41), channel_id=1, source_target_pairs={{0,0},{1,16},{2,32},{3,48},{4,64},{5,80},{6,96},{7,112},{8,128},{9... | collective-permute-start | bytes 49160 | tf_op jit(solution)/shard_map/ppermute | solution.py:127
  104.2 29.5 %all-to-all-start.4 = ((f32[16,16,256]{2,1,0:T(8,128)}), f32[16,16,256]{2,1,0:T(8,128)S(1)}, u32[]{:S(2)}, u32[]{:S(2)}) async-start(f32[16,16,256]{2,1,0:T(8,128)} %broadcast_in_dim.35), calls=%async_computation.4 | async-start | bytes 524288 | tf_op jit(solution)/shard_map/all_to_all | solution.py:38
  112.1 26.8 %copy-start.7 = (f32[16,16,256]{2,1,0:T(8,128)}, f32[16,16,256]{2,1,0:T(8,128)S(1)}, u32[]{:S(2)}) copy-start(f32[16,16,256]{2,1,0:T(8,128)S(1)} %get-tuple-element.37) | copy-start | bytes 786436
  134.9 19.1 %all-to-all-start.5 = ((f32[4,256,256]{1,2,0:T(8,128)}), f32[4,256,256]{1,2,0:T(8,128)S(1)}, u32[]{:S(2)}, u32[]{:S(2)}) async-start(f32[4,256,256]{1,2,0:T(8,128)} %broadcast_in_dim.72), calls=%async_computation.5 | async-start | bytes 2097152 | tf_op jit(solution)/shard_map/all_to_all | solution.py:38
  151.0 3.0 %copy-start.5 = (f32[256,256]{1,0:T(8,128)}, f32[256,256]{1,0:T(8,128)S(1)}, u32[]{:S(2)}) copy-start(f32[256,256]{1,0:T(8,128)S(1)} %get-tuple-element.45) | copy-start | bytes 786436
  154.0 3.2 %copy-start.2 = (f32[256,256]{0,1:T(8,128)}, f32[256,256]{0,1:T(8,128)S(1)}, u32[]{:S(2)}) copy-start(f32[256,256]{0,1:T(8,128)S(1)} %get-tuple-element.43) | copy-start | bytes 786436
  179.1 38.5 %copy-start.6 = (f32[256,256]{1,0:T(8,128)S(1)}, f32[256,256]{1,0:T(8,128)}, u32[]{:S(2)}) copy-start(f32[256,256]{1,0:T(8,128)} %copy-done.5) | copy-start | bytes 786436
  179.1 38.5 %copy-start.8 = (f32[16,16,256]{2,1,0:T(8,128)S(1)}, f32[16,16,256]{2,1,0:T(8,128)}, u32[]{:S(2)}) copy-start(f32[16,16,256]{2,1,0:T(8,128)} %copy-done.7) | copy-start | bytes 786436
  179.1 38.5 %copy-start.9 = (f32[16,16,256]{2,1,0:T(8,128)S(1)}, f32[16,16,256]{2,1,0:T(8,128)}, u32[]{:S(2)}) copy-start(f32[16,16,256]{2,1,0:T(8,128)} %get-tuple-element.35) | copy-start | bytes 786436
  179.9 31.3 %all-to-all-start.7 = ((f32[16,16,256]{2,1,0:T(8,128)}), f32[16,16,256]{2,1,0:T(8,128)S(1)}, u32[]{:S(2)}, u32[]{:S(2)}) async-start(f32[16,16,256]{2,1,0:T(8,128)} %broadcast_in_dim.73), calls=%async_computation.7 | async-start | bytes 524288 | tf_op jit(solution)/shard_map/all_to_all | solution.py:38
  191.7 15.5 %collective-permute-start.1 = (f32[16,256]{1,0:T(8,128)S(1)}, f32[16,256]{1,0:T(8,128)S(1)}, u32[]{:S(2)}, u32[]{:S(2)}) collective-permute-start(f32[16,256]{1,0:T(8,128)S(1)} %get-tuple-element.49), channel_id=1, source_target_pairs={{0,0},{1,16},{2,32},{3,48},{4,64},{5,80},{6,96},{7,112},{8,128},{9... | collective-permute-start | bytes 49160 | tf_op jit(solution)/shard_map/ppermute | solution.py:127
  211.9 23.3 %all-to-all-start.8 = ((f32[16,16,256]{2,1,0:T(8,128)}), f32[16,16,256]{2,1,0:T(8,128)S(1)}, u32[]{:S(2)}, u32[]{:S(2)}) async-start(f32[16,16,256]{2,1,0:T(8,128)} %broadcast_in_dim.74), calls=%async_computation.8 | async-start | bytes 524288 | tf_op jit(solution)/shard_map/all_to_all | solution.py:38
  236.3 21.4 %all-to-all-start.9 = ((f32[4,272,256]{2,1,0:T(8,128)}), f32[4,272,256]{2,1,0:T(8,128)S(1)}, u32[]{:S(2)}, u32[]{:S(2)}) async-start(f32[4,272,256]{2,1,0:T(8,128)} %broadcast_in_dim.75), calls=%async_computation.9 | async-start | bytes 2228224 | tf_op jit(solution)/shard_map/all_to_all | solution.py:38
  258.6 26.5 %all-to-all-start.10 = ((f32[16,32,256]{2,1,0:T(8,128)}), f32[16,32,256]{2,1,0:T(8,128)}, u32[]{:S(2)}, u32[]{:S(2)}) async-start(f32[16,32,256]{2,1,0:T(8,128)} %broadcast_in_dim.76), calls=%async_computation.10 | async-start | bytes 1048576 | tf_op jit(solution)/shard_map/all_to_all | solution.py:38
  267.9 0.9 copy-start.1
  267.9 1.0 copy-start.3
  286.2 1.4 copy-start.4

commit v3 on v2

--- a/solution.py
+++ b/solution.py
@@ -193,9 +193,5 @@
     shape = (mesh.shape["row"] // 2, 2, 4, mesh.shape["col"] // 4)
     torus = Mesh(mesh.devices.reshape(shape), EVERY)
     return jax.shard_map(
-        per_device,
-        mesh=torus,
-        in_specs=(P(ROW, COL),),
-        out_specs=P(ROW, COL),
-        check_vma=False,
+        per_device, mesh=torus, in_specs=(P(ROW, COL),), out_specs=P(ROW, COL), check_vma=False
     )

time: 291 us -> 291 us (level)
  no operation moved by 1% of the time
where the time goes in v3:
time: 291 us; the launch traced here: 290 us
  starting transfers between devices  74.5 us (26%)
  waiting for transfers between devices  69.4 us (24%)
  blocking collectives  53.3 us (18%)
  other arithmetic  35.1 us (12%)
  Pallas kernels  32.9 us (11%)
  local copies, waits for them, and re-layouts  11.6 us (4%)
  matrix products  11.3 us (4%)
    all_to_all x8, starting transfers between devices, exchange(): return lax.all_to_all(tiles, axis, 0, 0, tiled=True)  68.5 us
    all_to_all x3, blocking collectives, exchange(): return lax.all_to_all(tiles, axis, 0, 0, tiled=True)  53.3 us
    all_to_all x8, waiting for transfers between devices, exchange(): return lax.all_to_all(tiles, axis, 0, 0, tiled=True)  51 us
    another operation x6, other arithmetic, per_device(): low = lax.linalg.cholesky(gram, symmetrize_input=False)  34 us
    ppermute x2, waiting for transfers between devices, to_block_row(): return lax.ppermute(piece, EVERY, pairs)  18.3 us
    pallas_call x1, Pallas kernels, inverted(): pl.pallas_call(second_half, out_shape=jax.ShapeDtypeStruct((2 * h, 2 * h)...  16.5 us
    pallas_call x1, Pallas kernels, half_inverted(): pl.pallas_call(first_half, out_shape=[half] * 4, scratch_shapes=[pltpu.VM...  16.4 us
    dot_general x12, matrix products, dot(): lax.dot_general(left, right, (dims, ((), ())), precision=precision, prefe...  10.8 us
  transfers between devices with their start and end apart: 10, of which 7 were waited for; matrix products, arithmetic and copies ran while one was open for 13% of the time, Pallas kernels for 11%

profile of v3, /device:TPU:1, one launch (start us, length us, event | category | flops | bytes accessed | tf_op | source)
XLA Modules:
  0.0 289.8 jit_solution(17006016363945430068)
XLA Ops:
  0.0 3.0 %fusion = f32[256,256]{1,0:T(8,128)S(1)} fusion(f32[1024,256]{1,0:T(8,128)} %param.1), kind=kOutput, calls=%fused_computation.6 | convolution fusion | flops 603979776 | bytes 1048576 | tf_op jit(solution)/shard_map/dot_general | solution.py:16
  4.6 17.5 %all-to-all-start = ((f32[16,32,256]{2,1,0:T(8,128)}), f32[16,32,256]{2,1,0:T(8,128)S(1)}, u32[]{:S(2)}, u32[]{:S(2)}) async-start(f32[16,32,256]{2,1,0:T(8,128)} %pad_maximum_fusion), calls=%async_computation | async-start | bytes 1048576 | tf_op jit(solution)/shard_map/all_to_all | solution.py:38
  22.1 17.3 %all-to-all-done = f32[16,32,256]{2,1,0:T(8,128)S(1)} async-done(((f32[16,32,256]{2,1,0:T(8,128)}), f32[16,32,256]{2,1,0:T(8,128)S(1)}, u32[]{:S(2)}, u32[]{:S(2)}) %all-to-all-start) | async-done | bytes 524320 | tf_op jit(solution)/shard_map/all_to_all | solution.py:38
  39.5 6.8 %all_to_all.55 = f32[4,16,256]{2,1,0:T(8,128)S(1)} all-to-all(f32[4,16,256]{2,1,0:T(8,128)S(1)} %broadcast_in_dim.31), channel_id=1, replica_groups=mesh['y'=8,'core'=2,'x'=4,'z'=16] {'x'}, dimensions={0} | all-to-all | bytes 131072 | tf_op jit(solution)/shard_map/all_to_all | solution.py:38
  46.3 24.9 %all_to_all.56 = f32[16,16,256]{2,1,0:T(8,128)S(1)} all-to-all(f32[16,16,256]{2,1,0:T(8,128)S(1)} %broadcast_in_dim.33), channel_id=1, replica_groups=mesh['y'=8,'core'=2,'x'=4,'z'=16] {'z'}, dimensions={0} | all-to-all | bytes 524288 | tf_op jit(solution)/shard_map/all_to_all | solution.py:38
  72.2 8.5 %all-to-all-start.3 = ((f32[16,48,256]{2,1,0:T(8,128)}), f32[16,48,256]{2,1,0:T(8,128)S(1)}, u32[]{:S(2)}, u32[]{:S(2)}) async-start(f32[16,48,256]{2,1,0:T(8,128)} %broadcast_in_dim.34), calls=%async_computation.3 | async-start | bytes 1572864 | tf_op jit(solution)/shard_map/all_to_all | solution.py:38
  80.7 3.5 %collective-permute-start = (f32[16,256]{1,0:T(8,128)S(1)}, f32[16,256]{1,0:T(8,128)S(1)}, u32[]{:S(2)}, u32[]{:S(2)}) collective-permute-start(f32[16,256]{1,0:T(8,128)S(1)} %get-tuple-element.41), channel_id=1, source_target_pairs={{0,0},{1,16},{2,32},{3,48},{4,64},{5,80},{6,96},{7,112},{8,128},{9... | collective-permute-start | bytes 49160 | tf_op jit(solution)/shard_map/ppermute | solution.py:127
  84.3 5.4 %collective-permute-done = f32[16,256]{1,0:T(8,128)S(1)} collective-permute-done((f32[16,256]{1,0:T(8,128)S(1)}, f32[16,256]{1,0:T(8,128)S(1)}, u32[]{:S(2)}, u32[]{:S(2)}) %collective-permute-start) | collective-permute-done | bytes 16416 | tf_op jit(solution)/shard_map/ppermute | solution.py:127
  89.7 13.8 %all-to-all-done.3 = f32[16,48,256]{2,1,0:T(8,128)S(1)} async-done(((f32[16,48,256]{2,1,0:T(8,128)}), f32[16,48,256]{2,1,0:T(8,128)S(1)}, u32[]{:S(2)}, u32[]{:S(2)}) %all-to-all-start.3) | async-done | bytes 786464 | tf_op jit(solution)/shard_map/all_to_all | solution.py:38
  104.2 7.1 %all-to-all-start.4 = ((f32[16,16,256]{2,1,0:T(8,128)}), f32[16,16,256]{2,1,0:T(8,128)S(1)}, u32[]{:S(2)}, u32[]{:S(2)}) async-start(f32[16,16,256]{2,1,0:T(8,128)} %broadcast_in_dim.35), calls=%async_computation.4 | async-start | bytes 524288 | tf_op jit(solution)/shard_map/all_to_all | solution.py:38
  112.1 11.7 %cholesky.49 = f32[128,128]{1,0:T(8,128)S(1)} custom-call(f32[128,128]{1,0:T(8,128)S(1)} %cholesky.115), custom_call_target="Cholesky" | custom-call | tf_op jit(solution)/shard_map/cholesky | solution.py:155
  123.8 9.8 %custom-call.8 = f32[1,128,128]{1,2,0:T(8,128)S(1)} custom-call(f32[1,128,128]{2,1,0:T(8,128)S(1)} %get-tuple-element.47), custom_call_target="InvertDiagBlocksLowerTriangular" | custom-call | tf_op jit(solution)/shard_map/cholesky | solution.py:155
  134.9 3.7 %all-to-all-start.5 = ((f32[4,256,256]{1,2,0:T(8,128)}), f32[4,256,256]{1,2,0:T(8,128)S(1)}, u32[]{:S(2)}, u32[]{:S(2)}) async-start(f32[4,256,256]{1,2,0:T(8,128)} %broadcast_in_dim.72), calls=%async_computation.5 | async-start | bytes 2097152 | tf_op jit(solution)/shard_map/all_to_all | solution.py:38
  139.1 11.7 %cholesky.103 = f32[128,128]{1,0:T(8,128)S(1)} custom-call(f32[128,128]{1,0:T(8,128)S(1)} %convolution_subtract_fusion.3), custom_call_target="Cholesky" | custom-call | tf_op jit(solution)/shard_map/cholesky | solution.py:155
  157.6 21.5 %all_to_all.57 = f32[16,32,256]{2,1,0:T(8,128)S(1)} all-to-all(f32[16,32,256]{2,1,0:T(8,128)S(1)} %pad_maximum_fusion.1), channel_id=1, replica_groups=mesh['y'=8,'core'=2,'x'=4,'z'=16] {'y','core'}, dimensions={0} | all-to-all | bytes 1048576 | tf_op jit(solution)/shard_map/all_to_all | solution.py:38
  179.9 11.7 %all-to-all-start.7 = ((f32[16,16,256]{2,1,0:T(8,128)}), f32[16,16,256]{2,1,0:T(8,128)S(1)}, u32[]{:S(2)}, u32[]{:S(2)}) async-start(f32[16,16,256]{2,1,0:T(8,128)} %broadcast_in_dim.73), calls=%async_computation.7 | async-start | bytes 524288 | tf_op jit(solution)/shard_map/all_to_all | solution.py:38
  194.2 12.9 %collective-permute-done.1 = f32[16,256]{1,0:T(8,128)S(1)} collective-permute-done((f32[16,256]{1,0:T(8,128)S(1)}, f32[16,256]{1,0:T(8,128)S(1)}, u32[]{:S(2)}, u32[]{:S(2)}) %collective-permute-start.1) | collective-permute-done | bytes 16416 | tf_op jit(solution)/shard_map/ppermute | solution.py:127
  207.1 4.1 %all-to-all-done.7 = f32[16,16,256]{2,1,0:T(8,128)S(1)} async-done(((f32[16,16,256]{2,1,0:T(8,128)}), f32[16,16,256]{2,1,0:T(8,128)S(1)}, u32[]{:S(2)}, u32[]{:S(2)}) %all-to-all-start.7) | async-done | bytes 262176 | tf_op jit(solution)/shard_map/all_to_all | solution.py:38
  211.9 5.7 %all-to-all-start.8 = ((f32[16,16,256]{2,1,0:T(8,128)}), f32[16,16,256]{2,1,0:T(8,128)S(1)}, u32[]{:S(2)}, u32[]{:S(2)}) async-start(f32[16,16,256]{2,1,0:T(8,128)} %broadcast_in_dim.74), calls=%async_computation.8 | async-start | bytes 524288 | tf_op jit(solution)/shard_map/all_to_all | solution.py:38
  218.8 16.4 %shard_map.17 = (f32[128,128]{1,0:T(8,128)}, f32[128,128]{1,0:T(8,128)}, f32[128,128]{1,0:T(8,128)}, f32[128,128]{1,0:T(8,128)}) custom-call(f32[256,256]{1,0:T(8,128)} %convolution_add_fusion.a_ref), custom_call_target="tpu_custom_call" | custom-call | flops 2000000000 | bytes 500000 | tf_op jit(solution)/shard_map/pallas_call | solution.py:95
  236.3 4.9 %all-to-all-start.9 = ((f32[4,272,256]{2,1,0:T(8,128)}), f32[4,272,256]{2,1,0:T(8,128)S(1)}, u32[]{:S(2)}, u32[]{:S(2)}) async-start(f32[4,272,256]{2,1,0:T(8,128)} %broadcast_in_dim.75), calls=%async_computation.9 | async-start | bytes 2228224 | tf_op jit(solution)/shard_map/all_to_all | solution.py:38
  241.2 16.5 %shard_map.18 = f32[256,256]{1,0:T(8,128)} custom-call(f32[128,128]{1,0:T(8,128)} %get-tuple-element.29.t11_ref, f32[128,128]{1,0:T(8,128)} %get-tuple-element.30.right_ref, f32[128,128]{1,0:T(8,128)} %get-tuple-element.31.left_ref, f32[128,128]{1,0:T(8,128)} %get-tuple-element.32.schur_ref), custom_call_target="tpu_custom_call" | custom-call | flops 2000000000 | bytes 500000 | tf_op jit(solution)/shard_map/pallas_call | solution.py:105
  258.6 9.3 %all-to-all-start.10 = ((f32[16,32,256]{2,1,0:T(8,128)}), f32[16,32,256]{2,1,0:T(8,128)}, u32[]{:S(2)}, u32[]{:S(2)}) async-start(f32[16,32,256]{2,1,0:T(8,128)} %broadcast_in_dim.76), calls=%async_computation.10 | async-start | bytes 1048576 | tf_op jit(solution)/shard_map/all_to_all | solution.py:38
  270.1 15.0 %all-to-all-done.10 = f32[16,32,256]{2,1,0:T(8,128)} async-done(((f32[16,32,256]{2,1,0:T(8,128)}), f32[16,32,256]{2,1,0:T(8,128)}, u32[]{:S(2)}, u32[]{:S(2)}) %all-to-all-start.10) | async-done | bytes 524320 | tf_op jit(solution)/shard_map/all_to_all | solution.py:38
  (76 shorter events, 25.1 us)
Async XLA Ops:
  0.0 3.0 %copy-start = (f32[1024,256]{1,0:T(8,128)S(1)}, f32[1024,256]{1,0:T(8,128)}, u32[]{:S(2)}) copy-start(f32[1024,256]{1,0:T(8,128)} %param.1) | copy-start | bytes 3145732
  4.6 34.8 %all-to-all-start = ((f32[16,32,256]{2,1,0:T(8,128)}), f32[16,32,256]{2,1,0:T(8,128)S(1)}, u32[]{:S(2)}, u32[]{:S(2)}) async-start(f32[16,32,256]{2,1,0:T(8,128)} %pad_maximum_fusion), calls=%async_computation | async-start | bytes 1048576 | tf_op jit(solution)/shard_map/all_to_all | solution.py:38
  72.2 31.3 %all-to-all-start.3 = ((f32[16,48,256]{2,1,0:T(8,128)}), f32[16,48,256]{2,1,0:T(8,128)S(1)}, u32[]{:S(2)}, u32[]{:S(2)}) async-start(f32[16,48,256]{2,1,0:T(8,128)} %broadcast_in_dim.34), calls=%async_computation.3 | async-start | bytes 1572864 | tf_op jit(solution)/shard_map/all_to_all | solution.py:38
  80.7 9.0 %collective-permute-start = (f32[16,256]{1,0:T(8,128)S(1)}, f32[16,256]{1,0:T(8,128)S(1)}, u32[]{:S(2)}, u32[]{:S(2)}) collective-permute-start(f32[16,256]{1,0:T(8,128)S(1)} %get-tuple-element.41), channel_id=1, source_target_pairs={{0,0},{1,16},{2,32},{3,48},{4,64},{5,80},{6,96},{7,112},{8,128},{9... | collective-permute-start | bytes 49160 | tf_op jit(solution)/shard_map/ppermute | solution.py:127
  104.2 29.5 %all-to-all-start.4 = ((f32[16,16,256]{2,1,0:T(8,128)}), f32[16,16,256]{2,1,0:T(8,128)S(1)}, u32[]{:S(2)}, u32[]{:S(2)}) async-start(f32[16,16,256]{2,1,0:T(8,128)} %broadcast_in_dim.35), calls=%async_computation.4 | async-start | bytes 524288 | tf_op jit(solution)/shard_map/all_to_all | solution.py:38
  112.1 26.8 %copy-start.7 = (f32[16,16,256]{2,1,0:T(8,128)}, f32[16,16,256]{2,1,0:T(8,128)S(1)}, u32[]{:S(2)}) copy-start(f32[16,16,256]{2,1,0:T(8,128)S(1)} %get-tuple-element.37) | copy-start | bytes 786436
  134.9 19.1 %all-to-all-start.5 = ((f32[4,256,256]{1,2,0:T(8,128)}), f32[4,256,256]{1,2,0:T(8,128)S(1)}, u32[]{:S(2)}, u32[]{:S(2)}) async-start(f32[4,256,256]{1,2,0:T(8,128)} %broadcast_in_dim.72), calls=%async_computation.5 | async-start | bytes 2097152 | tf_op jit(solution)/shard_map/all_to_all | solution.py:38
  151.0 3.0 %copy-start.5 = (f32[256,256]{1,0:T(8,128)}, f32[256,256]{1,0:T(8,128)S(1)}, u32[]{:S(2)}) copy-start(f32[256,256]{1,0:T(8,128)S(1)} %get-tuple-element.45) | copy-start | bytes 786436
  154.0 3.2 %copy-start.2 = (f32[256,256]{0,1:T(8,128)}, f32[256,256]{0,1:T(8,128)S(1)}, u32[]{:S(2)}) copy-start(f32[256,256]{0,1:T(8,128)S(1)} %get-tuple-element.43) | copy-start | bytes 786436
  179.1 38.5 %copy-start.6 = (f32[256,256]{1,0:T(8,128)S(1)}, f32[256,256]{1,0:T(8,128)}, u32[]{:S(2)}) copy-start(f32[256,256]{1,0:T(8,128)} %copy-done.5) | copy-start | bytes 786436
  179.1 38.5 %copy-start.8 = (f32[16,16,256]{2,1,0:T(8,128)S(1)}, f32[16,16,256]{2,1,0:T(8,128)}, u32[]{:S(2)}) copy-start(f32[16,16,256]{2,1,0:T(8,128)} %copy-done.7) | copy-start | bytes 786436
  179.1 38.5 %copy-start.9 = (f32[16,16,256]{2,1,0:T(8,128)S(1)}, f32[16,16,256]{2,1,0:T(8,128)}, u32[]{:S(2)}) copy-start(f32[16,16,256]{2,1,0:T(8,128)} %get-tuple-element.35) | copy-start | bytes 786436
  179.9 31.3 %all-to-all-start.7 = ((f32[16,16,256]{2,1,0:T(8,128)}), f32[16,16,256]{2,1,0:T(8,128)S(1)}, u32[]{:S(2)}, u32[]{:S(2)}) async-start(f32[16,16,256]{2,1,0:T(8,128)} %broadcast_in_dim.73), calls=%async_computation.7 | async-start | bytes 524288 | tf_op jit(solution)/shard_map/all_to_all | solution.py:38
  191.7 15.5 %collective-permute-start.1 = (f32[16,256]{1,0:T(8,128)S(1)}, f32[16,256]{1,0:T(8,128)S(1)}, u32[]{:S(2)}, u32[]{:S(2)}) collective-permute-start(f32[16,256]{1,0:T(8,128)S(1)} %get-tuple-element.49), channel_id=1, source_target_pairs={{0,0},{1,16},{2,32},{3,48},{4,64},{5,80},{6,96},{7,112},{8,128},{9... | collective-permute-start | bytes 49160 | tf_op jit(solution)/shard_map/ppermute | solution.py:127
  211.9 23.3 %all-to-all-start.8 = ((f32[16,16,256]{2,1,0:T(8,128)}), f32[16,16,256]{2,1,0:T(8,128)S(1)}, u32[]{:S(2)}, u32[]{:S(2)}) async-start(f32[16,16,256]{2,1,0:T(8,128)} %broadcast_in_dim.74), calls=%async_computation.8 | async-start | bytes 524288 | tf_op jit(solution)/shard_map/all_to_all | solution.py:38
  236.3 21.4 %all-to-all-start.9 = ((f32[4,272,256]{2,1,0:T(8,128)}), f32[4,272,256]{2,1,0:T(8,128)S(1)}, u32[]{:S(2)}, u32[]{:S(2)}) async-start(f32[4,272,256]{2,1,0:T(8,128)} %broadcast_in_dim.75), calls=%async_computation.9 | async-start | bytes 2228224 | tf_op jit(solution)/shard_map/all_to_all | solution.py:38
  258.6 26.5 %all-to-all-start.10 = ((f32[16,32,256]{2,1,0:T(8,128)}), f32[16,32,256]{2,1,0:T(8,128)}, u32[]{:S(2)}, u32[]{:S(2)}) async-start(f32[16,32,256]{2,1,0:T(8,128)} %broadcast_in_dim.76), calls=%async_computation.10 | async-start | bytes 1048576 | tf_op jit(solution)/shard_map/all_to_all | solution.py:38
  267.9 0.9 copy-start.1
  267.9 1.0 copy-start.3
  286.2 1.4 copy-start.4

commit v4 on v3

--- a/solution.py
+++ b/solution.py
@@ -144,44 +144,36 @@
 
     lead = to_all(jnp.where(col_id == 0, gram_piece, piece), "x")[0]
     lead = to_all(lead, "z")[:2].reshape(2 * part, width)
-    lead = to_all(jnp.concatenate([lead, piece], axis=0), ROW)
+    lead = to_all(lead, ROW)
     lead, moved = lax.optimization_barrier((lead, moved))
     gram = lead[:, :part].reshape(width, width)
-    top = lead[:, part : 2 * part].reshape(width, width)
-    panel_c = lead[:, 2 * part :].reshape(width, width)
+    top = lead[:, part:].reshape(width, width)
 
     along_z = to_all(moved, "z").reshape(zs * part, width)
     panel_r = to_all(along_z, "x").reshape(row_count, width)
     low = lax.linalg.cholesky(gram, symmetrize_input=False)
     upper = SIGN * low.T
     parts = half_inverted(gram + SIGN * mm(low, top))
-    refl_c = panel_c + jnp.where(col_id == 1, upper, 0.0)
     refl_r = lax.dynamic_update_slice_in_dim(
         panel_r, panel_r[width : 2 * width] + first * upper, width, 0
     )
 
     x_part = tn(matrix, refl_r, fast)
-    y_part = tn(refl_c, x_part)
-    both = jnp.concatenate(
-        [x_part.reshape(rows, part, width), y_part.reshape(rows, part, width)], axis=1
-    )
-    both = jnp.sum(exchange(both, ROW), axis=0)
-    x_piece, y_piece = both[:part], both[part:]
+    x_piece = jnp.sum(exchange(x_part.reshape(rows, part, width), ROW), axis=0)
     x_moved = to_block_row(x_piece)
-    y_z = to_all(y_piece, "z")
-    x_moved, y_z = lax.optimization_barrier((x_moved, y_z))
-    y_z = jnp.sum(y_z, axis=0)
+    both = to_all(jnp.concatenate([x_piece, piece], axis=0), ROW)
+    x_moved, both = lax.optimization_barrier((x_moved, both))
+    x_c = both[:, :part].reshape(width, width)
+    refl_c = both[:, part:].reshape(width, width) + jnp.where(col_id == 1, upper, 0.0)
     x_z = to_all(x_moved, "z").reshape(zs * part, width)
-    both, parts = lax.optimization_barrier((jnp.concatenate([x_z, y_z], axis=0), parts))
-    both = to_all(both, "x")
+    x_z, parts = lax.optimization_barrier((x_z, parts))
+    x_r = to_all(x_z, "x").reshape(row_count, width)
     tfac = inverted(parts)
-    x_r = both[:, : zs * part].reshape(row_count, width)
-    y_piece = jnp.sum(both[:, zs * part :], axis=0)
-    both = jnp.concatenate([x_piece, y_piece], axis=0)
-    both, tfac = lax.optimization_barrier((both, tfac))
-    both = to_all(both, ROW)
-    x_c = both[:, :part].reshape(width, width)
-    y_full = both[:, part:].reshape(width, width)
+    x_r, tfac = lax.optimization_barrier((x_r, tfac))
+
+    y_part = tn(refl_r, x_r, fast)
+    y_piece = jnp.sum(exchange(y_part.reshape(rows, part, width), ROW), axis=0)
+    y_full = to_all(y_piece, ROW).reshape(width, width)
 
     middle = tn(tfac, mm(y_full, tfac))
     side = mm(x_c, tfac) - mm(refl_c, middle)

time: 291 us -> 286 us (0.983)
  waiting for transfers between devices: 69.4 us -> 58 us
  matrix products: 11.3 us -> 19.2 us
    dot_general x12, matrix products: 10.8 us -> 18.7 us  [dot(): lax.dot_general(left, right, (dims, ((), ())), precision=precision, prefe...]
    ppermute x2, waiting for transfers between devices: 18.3 us -> 11.5 us  [to_block_row(): return lax.ppermute(piece, EVERY, pairs)]
    all_to_all x8 -> x9, waiting for transfers between devices: 51 us -> 46.5 us  [exchange(): return lax.all_to_all(tiles, axis, 0, 0, tiled=True)]
    all_to_all x8 -> x9, starting transfers between devices: 68.5 us -> 66.9 us  [exchange(): return lax.all_to_all(tiles, axis, 0, 0, tiled=True)]
  transfers between devices with their start and end apart: 10 -> 11, of which waited for: 7 -> 7; matrix products, arithmetic and copies ran while one was open for 13% -> 17% of each run, Pallas kernels for 11% -> 12%
where the time goes in v4:
time: 286 us; the launch traced here: 285 us
  starting transfers between devices  73.3 us (26%)
  waiting for transfers between devices  58 us (20%)
  blocking collectives  50.9 us (18%)
  other arithmetic  35.9 us (13%)
  Pallas kernels  32.9 us (12%)
  matrix products  19.2 us (7%)
  local copies, waits for them, and re-layouts  12.9 us (5%)
    all_to_all x9, starting transfers between devices, exchange(): return lax.all_to_all(tiles, axis, 0, 0, tiled=True)  66.9 us
    all_to_all x3, blocking collectives, exchange(): return lax.all_to_all(tiles, axis, 0, 0, tiled=True)  50.9 us
    all_to_all x9, waiting for transfers between devices, exchange(): return lax.all_to_all(tiles, axis, 0, 0, tiled=True)  46.5 us
    another operation x6, other arithmetic, per_device(): low = lax.linalg.cholesky(gram, symmetrize_input=False)  34 us
    dot_general x12, matrix products, dot(): lax.dot_general(left, right, (dims, ((), ())), precision=precision, prefe...  18.7 us
    pallas_call x1, Pallas kernels, inverted(): pl.pallas_call(second_half, out_shape=jax.ShapeDtypeStruct((2 * h, 2 * h)...  16.5 us
    pallas_call x1, Pallas kernels, half_inverted(): pl.pallas_call(first_half, out_shape=[half] * 4, scratch_shapes=[pltpu.VM...  16.4 us
    ppermute x2, waiting for transfers between devices, to_block_row(): return lax.ppermute(piece, EVERY, pairs)  11.5 us
  transfers between devices with their start and end apart: 11, of which 7 were waited for; matrix products, arithmetic and copies ran while one was open for 17% of the time, Pallas kernels for 12%

profile of v4, /device:TPU:1, one launch (start us, length us, event | category | flops | bytes accessed | tf_op | source)
XLA Modules:
  0.0 284.6 jit_solution(1808272957606864982)
XLA Ops:
  4.6 17.5 %all-to-all-start = ((f32[16,32,256]{2,1,0:T(8,128)}), f32[16,32,256]{2,1,0:T(8,128)S(1)}, u32[]{:S(2)}, u32[]{:S(2)}) async-start(f32[16,32,256]{2,1,0:T(8,128)} %pad_maximum_fusion), calls=%async_computation | async-start | bytes 1048576 | tf_op jit(solution)/shard_map/all_to_all | solution.py:38
  22.1 17.3 %all-to-all-done = f32[16,32,256]{2,1,0:T(8,128)S(1)} async-done(((f32[16,32,256]{2,1,0:T(8,128)}), f32[16,32,256]{2,1,0:T(8,128)S(1)}, u32[]{:S(2)}, u32[]{:S(2)}) %all-to-all-start) | async-done | bytes 524320 | tf_op jit(solution)/shard_map/all_to_all | solution.py:38
  39.5 6.8 %all_to_all.60 = f32[4,16,256]{2,1,0:T(8,128)S(1)} all-to-all(f32[4,16,256]{2,1,0:T(8,128)S(1)} %broadcast_in_dim.33), channel_id=1, replica_groups=mesh['y'=8,'core'=2,'x'=4,'z'=16] {'x'}, dimensions={0} | all-to-all | bytes 131072 | tf_op jit(solution)/shard_map/all_to_all | solution.py:38
  46.3 24.9 %all_to_all.61 = f32[16,16,256]{2,1,0:T(8,128)S(1)} all-to-all(f32[16,16,256]{2,1,0:T(8,128)S(1)} %broadcast_in_dim.35), channel_id=1, replica_groups=mesh['y'=8,'core'=2,'x'=4,'z'=16] {'z'}, dimensions={0} | all-to-all | bytes 524288 | tf_op jit(solution)/shard_map/all_to_all | solution.py:38
  72.1 8.5 %all-to-all-start.3 = ((f32[16,32,256]{2,1,0:T(8,128)}), f32[16,32,256]{2,1,0:T(8,128)S(1)}, u32[]{:S(2)}, u32[]{:S(2)}) async-start(f32[16,32,256]{2,1,0:T(8,128)} %broadcast_in_dim.71), calls=%async_computation.3 | async-start | bytes 1048576 | tf_op jit(solution)/shard_map/all_to_all | solution.py:38
  80.6 3.5 %collective-permute-start = (f32[16,256]{1,0:T(8,128)S(1)}, f32[16,256]{1,0:T(8,128)S(1)}, u32[]{:S(2)}, u32[]{:S(2)}) collective-permute-start(f32[16,256]{1,0:T(8,128)S(1)} %get-tuple-element.39), channel_id=1, source_target_pairs={{0,0},{1,16},{2,32},{3,48},{4,64},{5,80},{6,96},{7,112},{8,128},{9... | collective-permute-start | bytes 49160 | tf_op jit(solution)/shard_map/ppermute | solution.py:127
  84.1 5.4 %collective-permute-done = f32[16,256]{1,0:T(8,128)S(1)} collective-permute-done((f32[16,256]{1,0:T(8,128)S(1)}, f32[16,256]{1,0:T(8,128)S(1)}, u32[]{:S(2)}, u32[]{:S(2)}) %collective-permute-start) | collective-permute-done | bytes 16416 | tf_op jit(solution)/shard_map/ppermute | solution.py:127
  89.5 8.4 %all-to-all-done.3 = f32[16,32,256]{2,1,0:T(8,128)S(1)} async-done(((f32[16,32,256]{2,1,0:T(8,128)}), f32[16,32,256]{2,1,0:T(8,128)S(1)}, u32[]{:S(2)}, u32[]{:S(2)}) %all-to-all-start.3) | async-done | bytes 524320 | tf_op jit(solution)/shard_map/all_to_all | solution.py:38
  98.6 7.2 %all-to-all-start.4 = ((f32[16,16,256]{2,1,0:T(8,128)}), f32[16,16,256]{2,1,0:T(8,128)S(1)}, u32[]{:S(2)}, u32[]{:S(2)}) async-start(f32[16,16,256]{2,1,0:T(8,128)} %broadcast_in_dim.72), calls=%async_computation.4 | async-start | bytes 524288 | tf_op jit(solution)/shard_map/all_to_all | solution.py:38
  106.6 11.7 %cholesky.49 = f32[128,128]{1,0:T(8,128)S(1)} custom-call(f32[128,128]{1,0:T(8,128)S(1)} %cholesky.115), custom_call_target="Cholesky" | custom-call | tf_op jit(solution)/shard_map/cholesky | solution.py:154
  118.3 9.8 %custom-call.8 = f32[1,128,128]{1,2,0:T(8,128)S(1)} custom-call(f32[1,128,128]{2,1,0:T(8,128)S(1)} %get-tuple-element.44), custom_call_target="InvertDiagBlocksLowerTriangular" | custom-call | tf_op jit(solution)/shard_map/cholesky | solution.py:154
  129.4 3.7 %all-to-all-start.5 = ((f32[4,256,256]{1,2,0:T(8,128)}), f32[4,256,256]{1,2,0:T(8,128)S(1)}, u32[]{:S(2)}, u32[]{:S(2)}) async-start(f32[4,256,256]{1,2,0:T(8,128)} %broadcast_in_dim.74), calls=%async_computation.5 | async-start | bytes 2097152 | tf_op jit(solution)/shard_map/all_to_all | solution.py:38
  133.6 11.7 %cholesky.103 = f32[128,128]{1,0:T(8,128)S(1)} custom-call(f32[128,128]{1,0:T(8,128)S(1)} %convolution_subtract_fusion.3), custom_call_target="Cholesky" | custom-call | tf_op jit(solution)/shard_map/cholesky | solution.py:154
  150.4 19.2 %all_to_all.62 = f32[16,16,256]{2,1,0:T(8,128)S(1)} all-to-all(f32[16,16,256]{2,1,0:T(8,128)S(1)} %bitcast.73), channel_id=1, replica_groups=mesh['y'=8,'core'=2,'x'=4,'z'=16] {'y','core'}, dimensions={0} | all-to-all | bytes 524288 | tf_op jit(solution)/shard_map/all_to_all | solution.py:38
  176.8 6.0 %collective-permute-done.1 = f32[16,256]{1,0:T(8,128)S(1)} collective-permute-done((f32[16,256]{1,0:T(8,128)S(1)}, f32[16,256]{1,0:T(8,128)S(1)}, u32[]{:S(2)}, u32[]{:S(2)}) %collective-permute-start.1) | collective-permute-done | bytes 16416 | tf_op jit(solution)/shard_map/ppermute | solution.py:127
  182.9 7.8 %all-to-all-done.7 = f32[16,32,256]{2,1,0:T(8,128)S(1)} async-done(((f32[16,32,256]{2,1,0:T(8,128)}), f32[16,32,256]{2,1,0:T(8,128)S(1)}, u32[]{:S(2)}, u32[]{:S(2)}) %all-to-all-start.7) | async-done | bytes 524320 | tf_op jit(solution)/shard_map/all_to_all | solution.py:38
  191.5 13.2 %all-to-all-start.8 = ((f32[16,16,256]{2,1,0:T(8,128)}), f32[16,16,256]{2,1,0:T(8,128)S(1)}, u32[]{:S(2)}, u32[]{:S(2)}) async-start(f32[16,16,256]{2,1,0:T(8,128)} %broadcast_in_dim.76), calls=%async_computation.8 | async-start | bytes 524288 | tf_op jit(solution)/shard_map/all_to_all | solution.py:38
  206.7 16.4 %shard_map.17 = (f32[128,128]{1,0:T(8,128)}, f32[128,128]{1,0:T(8,128)}, f32[128,128]{1,0:T(8,128)}, f32[128,128]{1,0:T(8,128)}) custom-call(f32[256,256]{1,0:T(8,128)} %convolution_add_fusion.a_ref), custom_call_target="tpu_custom_call" | custom-call | flops 2000000000 | bytes 500000 | tf_op jit(solution)/shard_map/pallas_call | solution.py:95
  224.2 3.5 %all-to-all-start.9 = ((f32[4,256,256]{2,1,0:T(8,128)}), f32[4,256,256]{2,1,0:T(8,128)S(1)}, u32[]{:S(2)}, u32[]{:S(2)}) async-start(f32[4,256,256]{2,1,0:T(8,128)} %broadcast_in_dim.77), calls=%async_computation.9 | async-start | bytes 2097152 | tf_op jit(solution)/shard_map/all_to_all | solution.py:38
  227.7 16.5 %shard_map.18 = f32[256,256]{1,0:T(8,128)} custom-call(f32[128,128]{1,0:T(8,128)} %get-tuple-element.28.t11_ref, f32[128,128]{1,0:T(8,128)} %get-tuple-element.29.right_ref, f32[128,128]{1,0:T(8,128)} %get-tuple-element.30.left_ref, f32[128,128]{1,0:T(8,128)} %get-tuple-element.31.schur_ref), custom_call_target="tpu_custom_call" | custom-call | flops 2000000000 | bytes 500000 | tf_op jit(solution)/shard_map/pallas_call | solution.py:105
  246.0 5.5 %all-to-all-start.10 = ((f32[16,16,256]{2,1,0:T(8,128)}), f32[16,16,256]{2,1,0:T(8,128)}, u32[]{:S(2)}, u32[]{:S(2)}) async-start(f32[16,16,256]{2,1,0:T(8,128)} %bitcast.72), calls=%async_computation.10 | async-start | bytes 524288 | tf_op jit(solution)/shard_map/all_to_all | solution.py:38
  257.4 5.7 %all-to-all-done.10 = f32[16,16,256]{2,1,0:T(8,128)} async-done(((f32[16,16,256]{2,1,0:T(8,128)}), f32[16,16,256]{2,1,0:T(8,128)}, u32[]{:S(2)}, u32[]{:S(2)}) %all-to-all-start.10) | async-done | bytes 262176 | tf_op jit(solution)/shard_map/all_to_all | solution.py:38
  264.8 4.3 %all-to-all-start.11 = ((f32[16,16,256]{2,1,0:T(8,128)}), f32[16,16,256]{2,1,0:T(8,128)}, u32[]{:S(2)}, u32[]{:S(2)}) async-start(f32[16,16,256]{2,1,0:T(8,128)} %broadcast_in_dim.78), calls=%async_computation.11 | async-start | bytes 524288 | tf_op jit(solution)/shard_map/all_to_all | solution.py:38
  272.9 7.3 %all-to-all-done.11 = f32[16,16,256]{2,1,0:T(8,128)} async-done(((f32[16,16,256]{2,1,0:T(8,128)}), f32[16,16,256]{2,1,0:T(8,128)}, u32[]{:S(2)}, u32[]{:S(2)}) %all-to-all-start.11) | async-done | bytes 262176 | tf_op jit(solution)/shard_map/all_to_all | solution.py:38
  (70 shorter events, 41.2 us)
Async XLA Ops:
  0.0 3.0 %copy-start = (f32[1024,256]{1,0:T(8,128)S(1)}, f32[1024,256]{1,0:T(8,128)}, u32[]{:S(2)}) copy-start(f32[1024,256]{1,0:T(8,128)} %param.1) | copy-start | bytes 3145732
  4.6 34.8 %all-to-all-start = ((f32[16,32,256]{2,1,0:T(8,128)}), f32[16,32,256]{2,1,0:T(8,128)S(1)}, u32[]{:S(2)}, u32[]{:S(2)}) async-start(f32[16,32,256]{2,1,0:T(8,128)} %pad_maximum_fusion), calls=%async_computation | async-start | bytes 1048576 | tf_op jit(solution)/shard_map/all_to_all | solution.py:38
  72.1 25.8 %all-to-all-start.3 = ((f32[16,32,256]{2,1,0:T(8,128)}), f32[16,32,256]{2,1,0:T(8,128)S(1)}, u32[]{:S(2)}, u32[]{:S(2)}) async-start(f32[16,32,256]{2,1,0:T(8,128)} %broadcast_in_dim.71), calls=%async_computation.3 | async-start | bytes 1048576 | tf_op jit(solution)/shard_map/all_to_all | solution.py:38
  80.6 9.0 %collective-permute-start = (f32[16,256]{1,0:T(8,128)S(1)}, f32[16,256]{1,0:T(8,128)S(1)}, u32[]{:S(2)}, u32[]{:S(2)}) collective-permute-start(f32[16,256]{1,0:T(8,128)S(1)} %get-tuple-element.39), channel_id=1, source_target_pairs={{0,0},{1,16},{2,32},{3,48},{4,64},{5,80},{6,96},{7,112},{8,128},{9... | collective-permute-start | bytes 49160 | tf_op jit(solution)/shard_map/ppermute | solution.py:127
  98.6 29.6 %all-to-all-start.4 = ((f32[16,16,256]{2,1,0:T(8,128)}), f32[16,16,256]{2,1,0:T(8,128)S(1)}, u32[]{:S(2)}, u32[]{:S(2)}) async-start(f32[16,16,256]{2,1,0:T(8,128)} %broadcast_in_dim.72), calls=%async_computation.4 | async-start | bytes 524288 | tf_op jit(solution)/shard_map/all_to_all | solution.py:38
  106.6 26.7 %copy-start.5 = (f32[16,16,256]{2,1,0:T(8,128)}, f32[16,16,256]{2,1,0:T(8,128)S(1)}, u32[]{:S(2)}) copy-start(f32[16,16,256]{2,1,0:T(8,128)S(1)} %get-tuple-element.38) | copy-start | bytes 786436
  129.4 17.8 %all-to-all-start.5 = ((f32[4,256,256]{1,2,0:T(8,128)}), f32[4,256,256]{1,2,0:T(8,128)S(1)}, u32[]{:S(2)}, u32[]{:S(2)}) async-start(f32[4,256,256]{1,2,0:T(8,128)} %broadcast_in_dim.74), calls=%async_computation.5 | async-start | bytes 2097152 | tf_op jit(solution)/shard_map/all_to_all | solution.py:38
  170.4 20.2 %all-to-all-start.7 = ((f32[16,32,256]{2,1,0:T(8,128)}), f32[16,32,256]{2,1,0:T(8,128)S(1)}, u32[]{:S(2)}, u32[]{:S(2)}) async-start(f32[16,32,256]{2,1,0:T(8,128)} %broadcast_in_dim.75), calls=%async_computation.7 | async-start | bytes 1048576 | tf_op jit(solution)/shard_map/all_to_all | solution.py:38
  173.9 9.0 %collective-permute-start.1 = (f32[16,256]{1,0:T(8,128)S(1)}, f32[16,256]{1,0:T(8,128)S(1)}, u32[]{:S(2)}, u32[]{:S(2)}) collective-permute-start(f32[16,256]{1,0:T(8,128)S(1)} %reduce_sum.31), channel_id=1, source_target_pairs={{0,0},{1,16},{2,32},{3,48},{4,64},{5,80},{6,96},{7,112},{8,128},{9... | collective-permute-start | bytes 49160 | tf_op jit(solution)/shard_map/ppermute | solution.py:127
  190.7 16.0 %copy-start.4 = (f32[16,32,256]{2,1,0:T(8,128)}, f32[16,32,256]{2,1,0:T(8,128)S(1)}, u32[]{:S(2)}) copy-start(f32[16,32,256]{2,1,0:T(8,128)S(1)} %all-to-all-done.7) | copy-start | bytes 1572868
  191.5 13.2 %copy-start.6 = (f32[16,16,256]{2,1,0:T(8,128)S(1)}, f32[16,16,256]{2,1,0:T(8,128)}, u32[]{:S(2)}) copy-start(f32[16,16,256]{2,1,0:T(8,128)} %copy-done.5) | copy-start | bytes 786436
  191.5 31.7 %all-to-all-start.8 = ((f32[16,16,256]{2,1,0:T(8,128)}), f32[16,16,256]{2,1,0:T(8,128)S(1)}, u32[]{:S(2)}, u32[]{:S(2)}) async-start(f32[16,16,256]{2,1,0:T(8,128)} %broadcast_in_dim.76), calls=%async_computation.8 | async-start | bytes 524288 | tf_op jit(solution)/shard_map/all_to_all | solution.py:38
  224.2 20.0 %all-to-all-start.9 = ((f32[4,256,256]{2,1,0:T(8,128)}), f32[4,256,256]{2,1,0:T(8,128)S(1)}, u32[]{:S(2)}, u32[]{:S(2)}) async-start(f32[4,256,256]{2,1,0:T(8,128)} %broadcast_in_dim.77), calls=%async_computation.9 | async-start | bytes 2097152 | tf_op jit(solution)/shard_map/all_to_all | solution.py:38
  246.0 17.2 %all-to-all-start.10 = ((f32[16,16,256]{2,1,0:T(8,128)}), f32[16,16,256]{2,1,0:T(8,128)}, u32[]{:S(2)}, u32[]{:S(2)}) async-start(f32[16,16,256]{2,1,0:T(8,128)} %bitcast.72), calls=%async_computation.10 | async-start | bytes 524288 | tf_op jit(solution)/shard_map/all_to_all | solution.py:38
  264.8 15.4 %all-to-all-start.11 = ((f32[16,16,256]{2,1,0:T(8,128)}), f32[16,16,256]{2,1,0:T(8,128)}, u32[]{:S(2)}, u32[]{:S(2)}) async-start(f32[16,16,256]{2,1,0:T(8,128)} %broadcast_in_dim.78), calls=%async_computation.11 | async-start | bytes 524288 | tf_op jit(solution)/shard_map/all_to_all | solution.py:38
  269.2 2.2 copy-start.8
  280.2 1.5 copy-start.1
  280.2 2.1 copy-start.3
  280.2 2.1 copy-start.7
  281.7 1.3 copy-start.2

commit v5 on v4

--- a/solution.py
+++ b/solution.py
@@ -140,9 +140,11 @@
     )
     piece = both[0, :part]
     gram_piece = jnp.sum(both[:, part:], axis=0)
-    moved = to_block_row(piece)
+    with jax.named_scope("move_panel"):
+        moved = to_block_row(piece)
 
-    lead = to_all(jnp.where(col_id == 0, gram_piece, piece), "x")[0]
+    with jax.named_scope("lead_x"):
+        lead = to_all(jnp.where(col_id == 0, gram_piece, piece), "x")[0]
     lead = to_all(lead, "z")[:2].reshape(2 * part, width)
     lead = to_all(lead, ROW)
     lead, moved = lax.optimization_barrier((lead, moved))
@@ -154,25 +156,32 @@
     low = lax.linalg.cholesky(gram, symmetrize_input=False)
     upper = SIGN * low.T
     parts = half_inverted(gram + SIGN * mm(low, top))
+    is_lead = jnp.logical_and(row_id == 0, lax.axis_index("x") == 1)
+    refl_z = along_z + jnp.where(is_lead, upper, 0.0)
     refl_r = lax.dynamic_update_slice_in_dim(
         panel_r, panel_r[width : 2 * width] + first * upper, width, 0
     )
 
     x_part = tn(matrix, refl_r, fast)
     x_piece = jnp.sum(exchange(x_part.reshape(rows, part, width), ROW), axis=0)
-    x_moved = to_block_row(x_piece)
-    both = to_all(jnp.concatenate([x_piece, piece], axis=0), ROW)
-    x_moved, both = lax.optimization_barrier((x_moved, both))
+    x_z = to_all(to_block_row(x_piece), "z").reshape(zs * part, width)
+
+    y_part = tn(refl_z, x_z, fast)
+    own = jnp.concatenate([x_piece, piece], axis=0)
+    own = jnp.broadcast_to(own[None], (rows, 2 * part, width))
+    both = jnp.concatenate([own, y_part.reshape(rows, part, width)], axis=1)
+    both, parts = lax.optimization_barrier((both, parts))
+    both = exchange(both, ROW)
+    tfac = inverted(parts)
     x_c = both[:, :part].reshape(width, width)
-    refl_c = both[:, part:].reshape(width, width) + jnp.where(col_id == 1, upper, 0.0)
-    x_z = to_all(x_moved, "z").reshape(zs * part, width)
-    x_z, parts = lax.optimization_barrier((x_z, parts))
-    x_r = to_all(x_z, "x").reshape(row_count, width)
-    tfac = inverted(parts)
-    x_r, tfac = lax.optimization_barrier((x_r, tfac))
+    panel_c = both[:, part : 2 * part].reshape(width, width)
+    refl_c = panel_c + jnp.where(col_id == 1, upper, 0.0)
+    y_piece = jnp.sum(both[:, 2 * part :], axis=0)
 
-    y_part = tn(refl_r, x_r, fast)
-    y_piece = jnp.sum(exchange(y_part.reshape(rows, part, width), ROW), axis=0)
+    both, tfac = lax.optimization_barrier((jnp.concatenate([x_z, y_piece], axis=0), tfac))
+    both = to_all(both, "x")
+    x_r = both[:, : zs * part].reshape(row_count, width)
+    y_piece = jnp.sum(both[:, zs * part :], axis=0)
     y_full = to_all(y_piece, ROW).reshape(width, width)
 
     middle = tn(tfac, mm(y_full, tfac))

time: 286 us -> 290 us (1.014)
  starting transfers between devices: 73.3 us -> 76.4 us
  waiting for transfers between devices: 58 us -> 61.1 us
    all_to_all x9 -> x8, starting transfers between devices: 66.9 us -> 70.1 us  [exchange(): return lax.all_to_all(tiles, axis, 0, 0, tiled=True)]
    all_to_all x9 -> x8, waiting for transfers between devices: 46.5 us -> 49.5 us  [exchange(): return lax.all_to_all(tiles, axis, 0, 0, tiled=True)]
    broadcast_in_dim x11 -> x10, local copies, waits for them, and re-layouts: 6.21 us -> 5.34 us  [to_all(): return exchange(jnp.broadcast_to(piece[None], (n, *piece.shape)), axis)]
  transfers between devices with their start and end apart: 11 -> 10, of which waited for: 7 -> 7; matrix products, arithmetic and copies ran while one was open for 17% -> 15% of each run, Pallas kernels for 12% -> 11%
where the time goes in v5:
time: 290 us; the launch traced here: 288 us
  starting transfers between devices  76.4 us (26%)
  waiting for transfers between devices  61.1 us (21%)
  blocking collectives  51 us (18%)
  other arithmetic  37.5 us (13%)
  Pallas kernels  33 us (11%)
  matrix products  16.5 us (6%)
  local copies, waits for them, and re-layouts  11.2 us (4%)
    all_to_all x8, starting transfers between devices, exchange(): return lax.all_to_all(tiles, axis, 0, 0, tiled=True)  70.1 us
    all_to_all x3, blocking collectives, exchange(): return lax.all_to_all(tiles, axis, 0, 0, tiled=True)  51 us
    all_to_all x8, waiting for transfers between devices, exchange(): return lax.all_to_all(tiles, axis, 0, 0, tiled=True)  49.5 us
    another operation x6, other arithmetic, per_device(): low = lax.linalg.cholesky(gram, symmetrize_input=False)  34 us
    pallas_call x1, Pallas kernels, inverted(): pl.pallas_call(second_half, out_shape=jax.ShapeDtypeStruct((2 * h, 2 * h)...  16.5 us
    pallas_call x1, Pallas kernels, half_inverted(): pl.pallas_call(first_half, out_shape=[half] * 4, scratch_shapes=[pltpu.VM...  16.5 us
    dot_general x12, matrix products, dot(): lax.dot_general(left, right, (dims, ((), ())), precision=precision, prefe...  16.1 us
    ppermute x2, waiting for transfers between devices, to_block_row(): return lax.ppermute(piece, EVERY, pairs)  11.6 us
  transfers between devices with their start and end apart: 10, of which 7 were waited for; matrix products, arithmetic and copies ran while one was open for 15% of the time, Pallas kernels for 11%

profile of v5, /device:TPU:1, one launch (start us, length us, event | category | flops | bytes accessed | tf_op | source)
XLA Modules:
  0.0 288.3 jit_solution(3707018881298039294)
XLA Ops:
  4.6 17.5 %all-to-all-start = ((f32[16,32,256]{2,1,0:T(8,128)}), f32[16,32,256]{2,1,0:T(8,128)S(1)}, u32[]{:S(2)}, u32[]{:S(2)}) async-start(f32[16,32,256]{2,1,0:T(8,128)} %pad_maximum_fusion.1), calls=%async_computation | async-start | bytes 1048576 | tf_op jit(solution)/shard_map/all_to_all | solution.py:38
  22.1 17.3 %all-to-all-done = f32[16,32,256]{2,1,0:T(8,128)S(1)} async-done(((f32[16,32,256]{2,1,0:T(8,128)}), f32[16,32,256]{2,1,0:T(8,128)S(1)}, u32[]{:S(2)}, u32[]{:S(2)}) %all-to-all-start) | async-done | bytes 524320 | tf_op jit(solution)/shard_map/all_to_all | solution.py:38
  39.5 6.8 %all_to_all.55 = f32[4,16,256]{2,1,0:T(8,128)S(1)} all-to-all(f32[4,16,256]{2,1,0:T(8,128)S(1)} %broadcast_in_dim.34), channel_id=1, replica_groups=mesh['y'=8,'core'=2,'x'=4,'z'=16] {'x'}, dimensions={0} | all-to-all | bytes 131072 | tf_op jit(solution)/shard_map/lead_x/all_to_all | solution.py:38
  46.3 24.9 %all_to_all.56 = f32[16,16,256]{2,1,0:T(8,128)S(1)} all-to-all(f32[16,16,256]{2,1,0:T(8,128)S(1)} %broadcast_in_dim.70), channel_id=1, replica_groups=mesh['y'=8,'core'=2,'x'=4,'z'=16] {'z'}, dimensions={0} | all-to-all | bytes 524288 | tf_op jit(solution)/shard_map/all_to_all | solution.py:38
  72.1 8.5 %all-to-all-start.3 = ((f32[16,32,256]{2,1,0:T(8,128)}), f32[16,32,256]{2,1,0:T(8,128)S(1)}, u32[]{:S(2)}, u32[]{:S(2)}) async-start(f32[16,32,256]{2,1,0:T(8,128)} %broadcast_in_dim.72), calls=%async_computation.3 | async-start | bytes 1048576 | tf_op jit(solution)/shard_map/all_to_all | solution.py:38
  80.6 3.5 %collective-permute-start = (f32[16,256]{1,0:T(8,128)S(1)}, f32[16,256]{1,0:T(8,128)S(1)}, u32[]{:S(2)}, u32[]{:S(2)}) collective-permute-start(f32[16,256]{1,0:T(8,128)S(1)} %get-tuple-element.36), channel_id=1, source_target_pairs={{0,0},{1,16},{2,32},{3,48},{4,64},{5,80},{6,96},{7,112},{8,128},{9... | collective-permute-start | bytes 49160 | tf_op jit(solution)/shard_map/move_panel/ppermute | solution.py:127
  84.1 5.4 %collective-permute-done = f32[16,256]{1,0:T(8,128)S(1)} collective-permute-done((f32[16,256]{1,0:T(8,128)S(1)}, f32[16,256]{1,0:T(8,128)S(1)}, u32[]{:S(2)}, u32[]{:S(2)}) %collective-permute-start) | collective-permute-done | bytes 16416 | tf_op jit(solution)/shard_map/move_panel/ppermute | solution.py:127
  89.5 8.4 %all-to-all-done.3 = f32[16,32,256]{2,1,0:T(8,128)S(1)} async-done(((f32[16,32,256]{2,1,0:T(8,128)}), f32[16,32,256]{2,1,0:T(8,128)S(1)}, u32[]{:S(2)}, u32[]{:S(2)}) %all-to-all-start.3) | async-done | bytes 524320 | tf_op jit(solution)/shard_map/all_to_all | solution.py:38
  98.6 7.2 %all-to-all-start.4 = ((f32[16,16,256]{2,1,0:T(8,128)}), f32[16,16,256]{2,1,0:T(8,128)S(1)}, u32[]{:S(2)}, u32[]{:S(2)}) async-start(f32[16,16,256]{2,1,0:T(8,128)} %broadcast_in_dim.73), calls=%async_computation.4 | async-start | bytes 524288 | tf_op jit(solution)/shard_map/all_to_all | solution.py:38
  106.6 11.7 %cholesky.49 = f32[128,128]{1,0:T(8,128)S(1)} custom-call(f32[128,128]{1,0:T(8,128)S(1)} %cholesky.115), custom_call_target="Cholesky" | custom-call | tf_op jit(solution)/shard_map/cholesky | solution.py:156
  118.3 9.8 %custom-call.8 = f32[1,128,128]{1,2,0:T(8,128)S(1)} custom-call(f32[1,128,128]{2,1,0:T(8,128)S(1)} %get-tuple-element.43), custom_call_target="InvertDiagBlocksLowerTriangular" | custom-call | tf_op jit(solution)/shard_map/cholesky | solution.py:156
  129.4 3.7 %all-to-all-start.5 = ((f32[4,256,256]{1,2,0:T(8,128)}), f32[4,256,256]{1,2,0:T(8,128)S(1)}, u32[]{:S(2)}, u32[]{:S(2)}) async-start(f32[4,256,256]{1,2,0:T(8,128)} %broadcast_in_dim.75), calls=%async_computation.5 | async-start | bytes 2097152 | tf_op jit(solution)/shard_map/all_to_all | solution.py:38
  133.6 11.7 %cholesky.103 = f32[128,128]{1,0:T(8,128)S(1)} custom-call(f32[128,128]{1,0:T(8,128)S(1)} %convolution_subtract_fusion.3), custom_call_target="Cholesky" | custom-call | tf_op jit(solution)/shard_map/cholesky | solution.py:156
  151.2 19.2 %all_to_all.57 = f32[16,16,256]{2,1,0:T(8,128)S(1)} all-to-all(f32[16,16,256]{2,1,0:T(8,128)S(1)} %bitcast.78), channel_id=1, replica_groups=mesh['y'=8,'core'=2,'x'=4,'z'=16] {'y','core'}, dimensions={0} | all-to-all | bytes 524288 | tf_op jit(solution)/shard_map/all_to_all | solution.py:38
  173.3 6.2 %collective-permute-done.1 = f32[16,256]{1,0:T(8,128)S(1)} collective-permute-done((f32[16,256]{1,0:T(8,128)S(1)}, f32[16,256]{1,0:T(8,128)S(1)}, u32[]{:S(2)}, u32[]{:S(2)}) %collective-permute-start.1) | collective-permute-done | bytes 16416 | tf_op jit(solution)/shard_map/ppermute | solution.py:127
  180.2 16.3 %all-to-all-start.7 = ((f32[16,16,256]{2,1,0:T(8,128)}), f32[16,16,256]{2,1,0:T(8,128)S(1)}, u32[]{:S(2)}, u32[]{:S(2)}) async-start(f32[16,16,256]{2,1,0:T(8,128)} %broadcast_in_dim.76), calls=%async_computation.7 | async-start | bytes 524288 | tf_op jit(solution)/shard_map/all_to_all | solution.py:38
  197.5 16.5 %shard_map.17 = (f32[128,128]{1,0:T(8,128)}, f32[128,128]{1,0:T(8,128)}, f32[128,128]{1,0:T(8,128)}, f32[128,128]{1,0:T(8,128)}) custom-call(f32[256,256]{1,0:T(8,128)} %convolution_add_fusion.a_ref), custom_call_target="tpu_custom_call" | custom-call | flops 2000000000 | bytes 500000 | tf_op jit(solution)/shard_map/pallas_call | solution.py:95
  215.3 8.7 %all-to-all-start.8 = ((f32[16,48,256]{2,1,0:T(8,128)}), f32[16,48,256]{2,1,0:T(8,128)S(1)}, u32[]{:S(2)}, u32[]{:S(2)}) async-start(f32[16,48,256]{2,1,0:T(8,128)} %pad_maximum_fusion), calls=%async_computation.8 | async-start | bytes 1572864 | tf_op jit(solution)/shard_map/all_to_all | solution.py:38
  224.0 16.5 %shard_map.18 = f32[256,256]{1,0:T(8,128)} custom-call(f32[128,128]{1,0:T(8,128)} %get-tuple-element.25.t11_ref, f32[128,128]{1,0:T(8,128)} %get-tuple-element.26.right_ref, f32[128,128]{1,0:T(8,128)} %get-tuple-element.27.left_ref, f32[128,128]{1,0:T(8,128)} %get-tuple-element.28.schur_ref), custom_call_target="tpu_custom_call" | custom-call | flops 2000000000 | bytes 500000 | tf_op jit(solution)/shard_map/pallas_call | solution.py:105
  240.5 6.3 %all-to-all-done.8 = f32[16,48,256]{2,1,0:T(8,128)S(1)} async-done(((f32[16,48,256]{2,1,0:T(8,128)}), f32[16,48,256]{2,1,0:T(8,128)S(1)}, u32[]{:S(2)}, u32[]{:S(2)}) %all-to-all-start.8) | async-done | bytes 786464 | tf_op jit(solution)/shard_map/all_to_all | solution.py:38
  248.8 3.5 %all-to-all-start.9 = ((f32[4,272,256]{2,1,0:T(8,128)}), f32[4,272,256]{2,1,0:T(8,128)S(1)}, u32[]{:S(2)}, u32[]{:S(2)}) async-start(f32[4,272,256]{2,1,0:T(8,128)} %broadcast_in_dim.78), calls=%async_computation.9 | async-start | bytes 2228224 | tf_op jit(solution)/shard_map/all_to_all | solution.py:38
  256.4 10.5 %all-to-all-done.9 = f32[4,272,256]{2,1,0:T(8,128)S(1)} async-done(((f32[4,272,256]{2,1,0:T(8,128)}), f32[4,272,256]{2,1,0:T(8,128)S(1)}, u32[]{:S(2)}, u32[]{:S(2)}) %all-to-all-start.9) | async-done | bytes 1114144 | tf_op jit(solution)/shard_map/all_to_all | solution.py:38
  267.7 4.7 %all-to-all-start.10 = ((f32[16,16,256]{2,1,0:T(8,128)}), f32[16,16,256]{2,1,0:T(8,128)}, u32[]{:S(2)}, u32[]{:S(2)}) async-start(f32[16,16,256]{2,1,0:T(8,128)} %broadcast_in_dim.79), calls=%async_computation.10 | async-start | bytes 524288 | tf_op jit(solution)/shard_map/all_to_all | solution.py:38
  277.1 7.0 %all-to-all-done.10 = f32[16,16,256]{2,1,0:T(8,128)} async-done(((f32[16,16,256]{2,1,0:T(8,128)}), f32[16,16,256]{2,1,0:T(8,128)}, u32[]{:S(2)}, u32[]{:S(2)}) %all-to-all-start.10) | async-done | bytes 262176 | tf_op jit(solution)/shard_map/all_to_all | solution.py:38
  (73 shorter events, 34.8 us)
Async XLA Ops:
  0.0 3.0 %copy-start = (f32[1024,256]{1,0:T(8,128)S(1)}, f32[1024,256]{1,0:T(8,128)}, u32[]{:S(2)}) copy-start(f32[1024,256]{1,0:T(8,128)} %param.1) | copy-start | bytes 3145732
  4.6 34.8 %all-to-all-start = ((f32[16,32,256]{2,1,0:T(8,128)}), f32[16,32,256]{2,1,0:T(8,128)S(1)}, u32[]{:S(2)}, u32[]{:S(2)}) async-start(f32[16,32,256]{2,1,0:T(8,128)} %pad_maximum_fusion.1), calls=%async_computation | async-start | bytes 1048576 | tf_op jit(solution)/shard_map/all_to_all | solution.py:38
  72.1 25.8 %all-to-all-start.3 = ((f32[16,32,256]{2,1,0:T(8,128)}), f32[16,32,256]{2,1,0:T(8,128)S(1)}, u32[]{:S(2)}, u32[]{:S(2)}) async-start(f32[16,32,256]{2,1,0:T(8,128)} %broadcast_in_dim.72), calls=%async_computation.3 | async-start | bytes 1048576 | tf_op jit(solution)/shard_map/all_to_all | solution.py:38
  80.6 9.0 %collective-permute-start = (f32[16,256]{1,0:T(8,128)S(1)}, f32[16,256]{1,0:T(8,128)S(1)}, u32[]{:S(2)}, u32[]{:S(2)}) collective-permute-start(f32[16,256]{1,0:T(8,128)S(1)} %get-tuple-element.36), channel_id=1, source_target_pairs={{0,0},{1,16},{2,32},{3,48},{4,64},{5,80},{6,96},{7,112},{8,128},{9... | collective-permute-start | bytes 49160 | tf_op jit(solution)/shard_map/move_panel/ppermute | solution.py:127
  98.6 29.6 %all-to-all-start.4 = ((f32[16,16,256]{2,1,0:T(8,128)}), f32[16,16,256]{2,1,0:T(8,128)S(1)}, u32[]{:S(2)}, u32[]{:S(2)}) async-start(f32[16,16,256]{2,1,0:T(8,128)} %broadcast_in_dim.73), calls=%async_computation.4 | async-start | bytes 524288 | tf_op jit(solution)/shard_map/all_to_all | solution.py:38
  106.6 26.7 %copy-start.4 = (f32[16,16,256]{2,1,0:T(8,128)}, f32[16,16,256]{2,1,0:T(8,128)S(1)}, u32[]{:S(2)}) copy-start(f32[16,16,256]{2,1,0:T(8,128)S(1)} %get-tuple-element.35) | copy-start | bytes 786436
  129.4 17.9 %all-to-all-start.5 = ((f32[4,256,256]{1,2,0:T(8,128)}), f32[4,256,256]{1,2,0:T(8,128)S(1)}, u32[]{:S(2)}, u32[]{:S(2)}) async-start(f32[4,256,256]{1,2,0:T(8,128)} %broadcast_in_dim.75), calls=%async_computation.5 | async-start | bytes 2097152 | tf_op jit(solution)/shard_map/all_to_all | solution.py:38
  151.2 45.2 %copy-start.5 = (f32[16,16,256]{2,1,0:T(8,128)S(1)}, f32[16,16,256]{2,1,0:T(8,128)}, u32[]{:S(2)}) copy-start(f32[16,16,256]{2,1,0:T(8,128)} %copy-done.4) | copy-start | bytes 786436
  151.2 45.2 %copy-start.8 = (f32[16,16,256]{2,1,0:T(8,128)S(1)}, f32[16,16,256]{2,1,0:T(8,128)}, u32[]{:S(2)}) copy-start(f32[16,16,256]{2,1,0:T(8,128)} %get-tuple-element.34) | copy-start | bytes 786436
  170.5 9.0 %collective-permute-start.1 = (f32[16,256]{1,0:T(8,128)S(1)}, f32[16,256]{1,0:T(8,128)S(1)}, u32[]{:S(2)}, u32[]{:S(2)}) collective-permute-start(f32[16,256]{1,0:T(8,128)S(1)} %reduce_sum.40), channel_id=1, source_target_pairs={{0,0},{1,16},{2,32},{3,48},{4,64},{5,80},{6,96},{7,112},{8,128},{9... | collective-permute-start | bytes 49160 | tf_op jit(solution)/shard_map/ppermute | solution.py:127
  180.2 33.9 %all-to-all-start.7 = ((f32[16,16,256]{2,1,0:T(8,128)}), f32[16,16,256]{2,1,0:T(8,128)S(1)}, u32[]{:S(2)}, u32[]{:S(2)}) async-start(f32[16,16,256]{2,1,0:T(8,128)} %broadcast_in_dim.76), calls=%async_computation.7 | async-start | bytes 524288 | tf_op jit(solution)/shard_map/all_to_all | solution.py:38
  197.5 16.5 %copy-start.6 = (f32[256,256]{0,1:T(8,128)S(1)}, f32[256,256]{0,1:T(8,128)}, u32[]{:S(2)}) copy-start(f32[256,256]{0,1:T(8,128)} %get-tuple-element.39) | copy-start | bytes 786436
  215.3 31.5 %all-to-all-start.8 = ((f32[16,48,256]{2,1,0:T(8,128)}), f32[16,48,256]{2,1,0:T(8,128)S(1)}, u32[]{:S(2)}, u32[]{:S(2)}) async-start(f32[16,48,256]{2,1,0:T(8,128)} %pad_maximum_fusion), calls=%async_computation.8 | async-start | bytes 1572864 | tf_op jit(solution)/shard_map/all_to_all | solution.py:38
  248.8 18.2 %all-to-all-start.9 = ((f32[4,272,256]{2,1,0:T(8,128)}), f32[4,272,256]{2,1,0:T(8,128)S(1)}, u32[]{:S(2)}, u32[]{:S(2)}) async-start(f32[4,272,256]{2,1,0:T(8,128)} %broadcast_in_dim.78), calls=%async_computation.9 | async-start | bytes 2228224 | tf_op jit(solution)/shard_map/all_to_all | solution.py:38
  267.7 16.4 %all-to-all-start.10 = ((f32[16,16,256]{2,1,0:T(8,128)}), f32[16,16,256]{2,1,0:T(8,128)}, u32[]{:S(2)}, u32[]{:S(2)}) async-start(f32[16,16,256]{2,1,0:T(8,128)} %broadcast_in_dim.79), calls=%async_computation.10 | async-start | bytes 524288 | tf_op jit(solution)/shard_map/all_to_all | solution.py:38
  274.5 0.9 copy-start.9
  275.5 8.6 %copy-start.1 = (f32[256,256]{1,0:T(8,128)S(1)}, f32[256,256]{1,0:T(8,128)}, u32[]{:S(2)}) copy-start(f32[256,256]{1,0:T(8,128)} %shard_map.18) | copy-start | bytes 786436
  277.0 9.0 %copy-start.3 = (f32[256,256]{0,1:T(8,128)S(1)}, f32[256,256]{0,1:T(8,128)}, u32[]{:S(2)}) copy-start(f32[256,256]{0,1:T(8,128)} %copy.17) | copy-start | bytes 786436
  277.1 9.0 %copy-start.7 = (f32[256,256]{1,0:T(8,128)S(1)}, f32[256,256]{1,0:T(8,128)}, u32[]{:S(2)}) copy-start(f32[256,256]{1,0:T(8,128)} %fusion.21) | copy-start | bytes 786436
  285.4 1.2 copy-start.2

commit v6 on v5

--- a/solution.py
+++ b/solution.py
@@ -110,6 +110,103 @@
     )(*parts)
 
 
+GROUP = 4
+
+
+def eliminate(m_ref, c_ref, u_ref):
+    n, w = m_ref.shape
+    lanes = lax.broadcasted_iota(jnp.int32, (n, n), 1)
+    subs = lax.broadcasted_iota(jnp.int32, (n, n), 0)
+
+    def wide(x):
+        return jnp.concatenate([x] * (w // n), axis=1)
+
+    def step(trip, carry):
+        k = trip * GROUP
+        square = m_ref[:, :n]
+        cols, rows = [], []
+        for j in range(GROUP):
+            col = jnp.sum(jnp.where(lanes == k + j, square, 0.0), axis=1, keepdims=True)
+            col = jnp.broadcast_to(col, (n, n))
+            cols.append(col)
+            c_ref[j] = col
+            rows.append(m_ref[pl.ds(k + j, 1), :])
+        for j in range(GROUP):
+            pivot = c_ref[j, pl.ds(k + j, 1), :]
+            scale = lax.rsqrt(pivot)
+            scale = scale * (1.5 - 0.5 * pivot * scale * scale)
+            cols[j] = cols[j] * scale
+            rows[j] = rows[j] * wide(scale)
+            u_ref[j] = cols[j]
+            for i in range(j + 1, GROUP):
+                factor = u_ref[j, pl.ds(k + i, 1), :]
+                cols[i] = cols[i] - cols[j] * factor
+                rows[i] = rows[i] - rows[j] * wide(factor)
+                if i == j + 1:
+                    c_ref[i] = cols[i]
+        rest = m_ref[...]
+        below = subs >= k + GROUP
+        for j in range(GROUP):
+            rest = rest - wide(jnp.where(below, cols[j], 0.0)) * rows[j]
+        m_ref[...] = rest
+        for j in range(GROUP):
+            m_ref[pl.ds(k + j, 1), :] = rows[j]
+        return carry
+
+    lax.fori_loop(0, n // GROUP, step, 0)
+
+
+def upper_part(x):
+    subs = lax.broadcasted_iota(jnp.int32, x.shape, 0)
+    lanes = lax.broadcasted_iota(jnp.int32, x.shape, 1)
+    return jnp.where(subs <= lanes, x, 0.0)
+
+
+def first_rows(g_ref, rows_ref, schur_ref, m_ref, c_ref, u_ref):
+    h = m_ref.shape[0]
+    m_ref[...] = g_ref[:h, :]
+    eliminate(m_ref, c_ref, u_ref)
+    right = m_ref[:, h:]
+    rows_ref[:, :h] = upper_part(m_ref[:, :h])
+    rows_ref[:, h:] = right
+    schur_ref[...] = g_ref[h:, h:] - tn(right, right)
+
+
+def last_rows(rows_ref, schur_ref, out_ref, m_ref, c_ref, u_ref):
+    h = m_ref.shape[0]
+    m_ref[...] = schur_ref[...]
+    eliminate(m_ref, c_ref, u_ref)
+    out_ref[:h, :] = rows_ref[...]
+    out_ref[h:, :h] = jnp.zeros((h, h), jnp.float32)
+    out_ref[h:, h:] = upper_part(m_ref[...])
+
+
+def half_factored(gram):
+    n = gram.shape[0]
+    h = n // 2
+    return pl.pallas_call(
+        first_rows,
+        out_shape=[
+            jax.ShapeDtypeStruct((h, n), jnp.float32),
+            jax.ShapeDtypeStruct((h, h), jnp.float32),
+        ],
+        scratch_shapes=[pltpu.VMEM((h, n), jnp.float32)]
+        + [pltpu.VMEM((GROUP, h, h), jnp.float32)] * 2,
+        cost_estimate=COST,
+    )(gram)
+
+
+def factored(rows, schur):
+    h, n = rows.shape
+    return pl.pallas_call(
+        last_rows,
+        out_shape=jax.ShapeDtypeStruct((n, n), jnp.float32),
+        scratch_shapes=[pltpu.VMEM((h, h), jnp.float32)]
+        + [pltpu.VMEM((GROUP, h, h), jnp.float32)] * 2,
+        cost_estimate=COST,
+    )(rows, schur)
+
+
 def per_device(matrix):
     row_count, width = matrix.shape
     rows, xs, zs = lax.axis_size(ROW), lax.axis_size("x"), lax.axis_size("z")
@@ -152,10 +249,13 @@
     top = lead[:, part:].reshape(width, width)
 
     along_z = to_all(moved, "z").reshape(zs * part, width)
+    halves = half_factored(gram)
+    along_z, halves = lax.optimization_barrier((along_z, halves))
     panel_r = to_all(along_z, "x").reshape(row_count, width)
-    low = lax.linalg.cholesky(gram, symmetrize_input=False)
-    upper = SIGN * low.T
-    parts = half_inverted(gram + SIGN * mm(low, top))
+    factor = factored(*halves)
+    panel_r, factor = lax.optimization_barrier((panel_r, factor))
+    upper = SIGN * factor
+    parts = half_inverted(gram + tn(upper, top))
     is_lead = jnp.logical_and(row_id == 0, lax.axis_index("x") == 1)
     refl_z = along_z + jnp.where(is_lead, upper, 0.0)
     refl_r = lax.dynamic_update_slice_in_dim(

time: 290 us -> 279 us (0.962)
  other arithmetic: 37.5 us -> 5.51 us
  Pallas kernels: 33 us -> 54.9 us
  blocking collectives: 51 us -> 56.6 us
  local copies, waits for them, and re-layouts: 11.2 us -> 6.35 us
    another operation x6 -> x0, other arithmetic: 34 us -> none  [per_device(): low = lax.linalg.cholesky(gram, symmetrize_input=False)]
    pallas_call x0 -> x2, Pallas kernels: none -> 22 us  [the longest x1 11.4 us: half_factored(): pl.pallas_call(first_rows, out_shape=[jax.ShapeDtypeStruct((h, n), jnp.fl...]
    all_to_all x3, blocking collectives: 51 us -> 56.6 us  [exchange(): return lax.all_to_all(tiles, axis, 0, 0, tiled=True)]
    all_to_all x8, waiting for transfers between devices: 49.5 us -> 53.9 us  [exchange(): return lax.all_to_all(tiles, axis, 0, 0, tiled=True)]
  transfers between devices with their start and end apart: 10 -> 10, of which waited for: 7 -> 8; matrix products, arithmetic and copies ran while one was open for 15% -> 3% of each run, Pallas kernels for 11% -> 20%
where the time goes in v6:
time: 279 us; the launch traced here: 278 us
  starting transfers between devices  76.5 us (27%)
  waiting for transfers between devices  62.8 us (23%)
  blocking collectives  56.6 us (20%)
  Pallas kernels  54.9 us (20%)
  matrix products  14.9 us (5%)
  local copies, waits for them, and re-layouts  6.35 us (2%)
  other arithmetic  5.51 us (2%)
    all_to_all x8, starting transfers between devices, exchange(): return lax.all_to_all(tiles, axis, 0, 0, tiled=True)  67.5 us
    all_to_all x3, blocking collectives, exchange(): return lax.all_to_all(tiles, axis, 0, 0, tiled=True)  56.6 us
    all_to_all x8, waiting for transfers between devices, exchange(): return lax.all_to_all(tiles, axis, 0, 0, tiled=True)  53.9 us
    pallas_call x1, Pallas kernels, inverted(): pl.pallas_call(second_half, out_shape=jax.ShapeDtypeStruct((2 * h, 2 * h)...  16.5 us
    pallas_call x1, Pallas kernels, half_inverted(): pl.pallas_call(first_half, out_shape=[half] * 4, scratch_shapes=[pltpu.VM...  16.4 us
    dot_general x12, matrix products, dot(): lax.dot_general(left, right, (dims, ((), ())), precision=precision, prefe...  14.9 us
    pallas_call x1, Pallas kernels, half_factored(): pl.pallas_call(first_rows, out_shape=[jax.ShapeDtypeStruct((h, n), jnp.fl...  11.4 us
    pallas_call x1, Pallas kernels, factored(): pl.pallas_call(last_rows, out_shape=jax.ShapeDtypeStruct((n, n), jnp.floa...  10.5 us
  transfers between devices with their start and end apart: 10, of which 8 were waited for; matrix products, arithmetic and copies ran while one was open for 3% of the time, Pallas kernels for 20%

profile of v6, /device:TPU:1, one launch (start us, length us, event | category | flops | bytes accessed | tf_op | source)
XLA Modules:
  0.0 277.8 jit_solution(15575603798031832958)
XLA Ops:
  4.5 17.5 %all-to-all-start = ((f32[16,32,256]{2,1,0:T(8,128)}), f32[16,32,256]{2,1,0:T(8,128)S(1)}, u32[]{:S(2)}, u32[]{:S(2)}) async-start(f32[16,32,256]{2,1,0:T(8,128)} %pad_maximum_fusion.1), calls=%async_computation | async-start | bytes 1048576 | tf_op jit(solution)/shard_map/all_to_all | solution.py:38
  22.0 17.3 %all-to-all-done = f32[16,32,256]{2,1,0:T(8,128)S(1)} async-done(((f32[16,32,256]{2,1,0:T(8,128)}), f32[16,32,256]{2,1,0:T(8,128)S(1)}, u32[]{:S(2)}, u32[]{:S(2)}) %all-to-all-start) | async-done | bytes 524320 | tf_op jit(solution)/shard_map/all_to_all | solution.py:38
  39.3 6.8 %all_to_all.55 = f32[4,16,256]{2,1,0:T(8,128)S(1)} all-to-all(f32[4,16,256]{2,1,0:T(8,128)S(1)} %broadcast_in_dim.32), channel_id=1, replica_groups=mesh['y'=8,'core'=2,'x'=4,'z'=16] {'x'}, dimensions={0} | all-to-all | bytes 131072 | tf_op jit(solution)/shard_map/lead_x/all_to_all | solution.py:38
  46.2 24.9 %all_to_all.56 = f32[16,16,256]{2,1,0:T(8,128)S(1)} all-to-all(f32[16,16,256]{2,1,0:T(8,128)S(1)} %broadcast_in_dim.34), channel_id=1, replica_groups=mesh['y'=8,'core'=2,'x'=4,'z'=16] {'z'}, dimensions={0} | all-to-all | bytes 524288 | tf_op jit(solution)/shard_map/all_to_all | solution.py:38
  71.9 8.5 %all-to-all-start.3 = ((f32[16,32,256]{2,1,0:T(8,128)}), f32[16,32,256]{2,1,0:T(8,128)S(1)}, u32[]{:S(2)}, u32[]{:S(2)}) async-start(f32[16,32,256]{2,1,0:T(8,128)} %broadcast_in_dim.70), calls=%async_computation.3 | async-start | bytes 1048576 | tf_op jit(solution)/shard_map/all_to_all | solution.py:38
  80.4 3.5 %collective-permute-start = (f32[16,256]{1,0:T(8,128)S(1)}, f32[16,256]{1,0:T(8,128)S(1)}, u32[]{:S(2)}, u32[]{:S(2)}) collective-permute-start(f32[16,256]{1,0:T(8,128)S(1)} %get-tuple-element.50), channel_id=1, source_target_pairs={{0,0},{1,16},{2,32},{3,48},{4,64},{5,80},{6,96},{7,112},{8,128},{9... | collective-permute-start | bytes 49160 | tf_op jit(solution)/shard_map/move_panel/ppermute | solution.py:224
  84.0 5.4 %collective-permute-done = f32[16,256]{1,0:T(8,128)S(1)} collective-permute-done((f32[16,256]{1,0:T(8,128)S(1)}, f32[16,256]{1,0:T(8,128)S(1)}, u32[]{:S(2)}, u32[]{:S(2)}) %collective-permute-start) | collective-permute-done | bytes 16416 | tf_op jit(solution)/shard_map/move_panel/ppermute | solution.py:224
  89.4 8.4 %all-to-all-done.3 = f32[16,32,256]{2,1,0:T(8,128)S(1)} async-done(((f32[16,32,256]{2,1,0:T(8,128)}), f32[16,32,256]{2,1,0:T(8,128)S(1)}, u32[]{:S(2)}, u32[]{:S(2)}) %all-to-all-start.3) | async-done | bytes 524320 | tf_op jit(solution)/shard_map/all_to_all | solution.py:38
  98.5 7.2 %all-to-all-start.4 = ((f32[16,16,256]{2,1,0:T(8,128)}), f32[16,16,256]{2,1,0:T(8,128)S(1)}, u32[]{:S(2)}, u32[]{:S(2)}) async-start(f32[16,16,256]{2,1,0:T(8,128)} %broadcast_in_dim.71), calls=%async_computation.4 | async-start | bytes 524288 | tf_op jit(solution)/shard_map/all_to_all | solution.py:38
  106.4 11.4 %shard_map.17 = (f32[128,256]{1,0:T(8,128)}, f32[128,128]{1,0:T(8,128)}) custom-call(f32[256,256]{1,0:T(8,128)} %bitcast.64), custom_call_target="tpu_custom_call" | custom-call | flops 2000000000 | bytes 500000 | tf_op jit(solution)/shard_map/pallas_call | solution.py:187
  120.5 3.5 %all-to-all-start.5 = ((f32[4,256,256]{2,1,0:T(8,128)}), f32[4,256,256]{2,1,0:T(8,128)S(1)}, u32[]{:S(2)}, u32[]{:S(2)}) async-start(f32[4,256,256]{2,1,0:T(8,128)} %broadcast_in_dim.72), calls=%async_computation.5 | async-start | bytes 2097152 | tf_op jit(solution)/shard_map/all_to_all | solution.py:38
  124.1 10.5 %shard_map.18 = f32[256,256]{1,0:T(8,128)} custom-call(f32[128,256]{1,0:T(8,128)} %get-tuple-element.30.rows_ref, f32[128,128]{1,0:T(8,128)} %get-tuple-element.31.schur_ref), custom_call_target="tpu_custom_call" | custom-call | flops 2000000000 | bytes 500000 | tf_op jit(solution)/shard_map/pallas_call | solution.py:201
  136.7 24.9 %all_to_all.57 = f32[16,16,256]{2,1,0:T(8,128)S(1)} all-to-all(f32[16,16,256]{2,1,0:T(8,128)S(1)} %bitcast.60), channel_id=1, replica_groups=mesh['y'=8,'core'=2,'x'=4,'z'=16] {'y','core'}, dimensions={0} | all-to-all | bytes 524288 | tf_op jit(solution)/shard_map/all_to_all | solution.py:38
  161.6 5.5 %collective-permute-start.1 = (f32[16,256]{1,0:T(8,128)S(1)}, f32[16,256]{1,0:T(8,128)S(1)}, u32[]{:S(2)}, u32[]{:S(2)}) collective-permute-start(f32[16,256]{1,0:T(8,128)S(1)} %reduce_sum.40), channel_id=1, source_target_pairs={{0,0},{1,16},{2,32},{3,48},{4,64},{5,80},{6,96},{7,112},{8,128},{9... | collective-permute-start | bytes 49160 | tf_op jit(solution)/shard_map/ppermute | solution.py:224
  167.1 3.5 %collective-permute-done.1 = f32[16,256]{1,0:T(8,128)S(1)} collective-permute-done((f32[16,256]{1,0:T(8,128)S(1)}, f32[16,256]{1,0:T(8,128)S(1)}, u32[]{:S(2)}, u32[]{:S(2)}) %collective-permute-start.1) | collective-permute-done | bytes 16416 | tf_op jit(solution)/shard_map/ppermute | solution.py:224
  171.3 15.7 %all-to-all-start.7 = ((f32[16,16,256]{2,1,0:T(8,128)}), f32[16,16,256]{2,1,0:T(8,128)S(1)}, u32[]{:S(2)}, u32[]{:S(2)}) async-start(f32[16,16,256]{2,1,0:T(8,128)} %broadcast_in_dim.73), calls=%async_computation.7 | async-start | bytes 524288 | tf_op jit(solution)/shard_map/all_to_all | solution.py:38
  189.4 16.4 %shard_map.19 = (f32[128,128]{1,0:T(8,128)}, f32[128,128]{1,0:T(8,128)}, f32[128,128]{1,0:T(8,128)}, f32[128,128]{1,0:T(8,128)}) custom-call(f32[256,256]{1,0:T(8,128)} %convolution_add_fusion.a_ref), custom_call_target="tpu_custom_call" | custom-call | flops 2000000000 | bytes 500000 | tf_op jit(solution)/shard_map/pallas_call | solution.py:95
  207.1 6.6 %all-to-all-start.8 = ((f32[16,48,256]{2,1,0:T(8,128)}), f32[16,48,256]{2,1,0:T(8,128)S(1)}, u32[]{:S(2)}, u32[]{:S(2)}) async-start(f32[16,48,256]{2,1,0:T(8,128)} %pad_maximum_fusion), calls=%async_computation.8 | async-start | bytes 1572864 | tf_op jit(solution)/shard_map/all_to_all | solution.py:38
  213.7 16.5 %shard_map.20 = f32[256,256]{1,0:T(8,128)} custom-call(f32[128,128]{1,0:T(8,128)} %get-tuple-element.39.t11_ref, f32[128,128]{1,0:T(8,128)} %get-tuple-element.40.right_ref, f32[128,128]{1,0:T(8,128)} %get-tuple-element.41.left_ref, f32[128,128]{1,0:T(8,128)} %get-tuple-element.42.schur_ref), custom_call_target="tpu_custom_call" | custom-call | flops 2000000000 | bytes 500000 | tf_op jit(solution)/shard_map/pallas_call | solution.py:105
  230.1 6.3 %all-to-all-done.8 = f32[16,48,256]{2,1,0:T(8,128)S(1)} async-done(((f32[16,48,256]{2,1,0:T(8,128)}), f32[16,48,256]{2,1,0:T(8,128)S(1)}, u32[]{:S(2)}, u32[]{:S(2)}) %all-to-all-start.8) | async-done | bytes 786464 | tf_op jit(solution)/shard_map/all_to_all | solution.py:38
  238.4 3.7 %all-to-all-start.9 = ((f32[4,272,256]{2,1,0:T(8,128)}), f32[4,272,256]{2,1,0:T(8,128)S(1)}, u32[]{:S(2)}, u32[]{:S(2)}) async-start(f32[4,272,256]{2,1,0:T(8,128)} %broadcast_in_dim.75), calls=%async_computation.9 | async-start | bytes 2228224 | tf_op jit(solution)/shard_map/all_to_all | solution.py:38
  245.8 10.7 %all-to-all-done.9 = f32[4,272,256]{2,1,0:T(8,128)S(1)} async-done(((f32[4,272,256]{2,1,0:T(8,128)}), f32[4,272,256]{2,1,0:T(8,128)S(1)}, u32[]{:S(2)}, u32[]{:S(2)}) %all-to-all-start.9) | async-done | bytes 1114144 | tf_op jit(solution)/shard_map/all_to_all | solution.py:38
  257.2 4.9 %all-to-all-start.10 = ((f32[16,16,256]{2,1,0:T(8,128)}), f32[16,16,256]{2,1,0:T(8,128)}, u32[]{:S(2)}, u32[]{:S(2)}) async-start(f32[16,16,256]{2,1,0:T(8,128)} %broadcast_in_dim.76), calls=%async_computation.10 | async-start | bytes 524288 | tf_op jit(solution)/shard_map/all_to_all | solution.py:38
  264.3 9.6 %all-to-all-done.10 = f32[16,16,256]{2,1,0:T(8,128)} async-done(((f32[16,16,256]{2,1,0:T(8,128)}), f32[16,16,256]{2,1,0:T(8,128)}, u32[]{:S(2)}, u32[]{:S(2)}) %all-to-all-start.10) | async-done | bytes 262176 | tf_op jit(solution)/shard_map/all_to_all | solution.py:38
  (52 shorter events, 28.3 us)
Async XLA Ops:
  0.0 2.9 %copy-start = (f32[1024,256]{1,0:T(8,128)S(1)}, f32[1024,256]{1,0:T(8,128)}, u32[]{:S(2)}) copy-start(f32[1024,256]{1,0:T(8,128)} %param.1) | copy-start | bytes 3145732
  4.5 34.8 %all-to-all-start = ((f32[16,32,256]{2,1,0:T(8,128)}), f32[16,32,256]{2,1,0:T(8,128)S(1)}, u32[]{:S(2)}, u32[]{:S(2)}) async-start(f32[16,32,256]{2,1,0:T(8,128)} %pad_maximum_fusion.1), calls=%async_computation | async-start | bytes 1048576 | tf_op jit(solution)/shard_map/all_to_all | solution.py:38
  71.9 25.8 %all-to-all-start.3 = ((f32[16,32,256]{2,1,0:T(8,128)}), f32[16,32,256]{2,1,0:T(8,128)S(1)}, u32[]{:S(2)}, u32[]{:S(2)}) async-start(f32[16,32,256]{2,1,0:T(8,128)} %broadcast_in_dim.70), calls=%async_computation.3 | async-start | bytes 1048576 | tf_op jit(solution)/shard_map/all_to_all | solution.py:38
  80.4 9.0 %collective-permute-start = (f32[16,256]{1,0:T(8,128)S(1)}, f32[16,256]{1,0:T(8,128)S(1)}, u32[]{:S(2)}, u32[]{:S(2)}) collective-permute-start(f32[16,256]{1,0:T(8,128)S(1)} %get-tuple-element.50), channel_id=1, source_target_pairs={{0,0},{1,16},{2,32},{3,48},{4,64},{5,80},{6,96},{7,112},{8,128},{9... | collective-permute-start | bytes 49160 | tf_op jit(solution)/shard_map/move_panel/ppermute | solution.py:224
  98.5 21.0 %all-to-all-start.4 = ((f32[16,16,256]{2,1,0:T(8,128)}), f32[16,16,256]{2,1,0:T(8,128)S(1)}, u32[]{:S(2)}, u32[]{:S(2)}) async-start(f32[16,16,256]{2,1,0:T(8,128)} %broadcast_in_dim.71), calls=%async_computation.4 | async-start | bytes 524288 | tf_op jit(solution)/shard_map/all_to_all | solution.py:38
  120.5 14.1 %all-to-all-start.5 = ((f32[4,256,256]{2,1,0:T(8,128)}), f32[4,256,256]{2,1,0:T(8,128)S(1)}, u32[]{:S(2)}, u32[]{:S(2)}) async-start(f32[4,256,256]{2,1,0:T(8,128)} %broadcast_in_dim.72), calls=%async_computation.5 | async-start | bytes 2097152 | tf_op jit(solution)/shard_map/all_to_all | solution.py:38
  136.7 50.4 %copy-start.3 = (f32[256,256]{1,0:T(8,128)S(1)}, f32[256,256]{1,0:T(8,128)}, u32[]{:S(2)}) copy-start(f32[256,256]{1,0:T(8,128)} %shard_map.18) | copy-start | bytes 786436
  161.6 9.0 %collective-permute-start.1 = (f32[16,256]{1,0:T(8,128)S(1)}, f32[16,256]{1,0:T(8,128)S(1)}, u32[]{:S(2)}, u32[]{:S(2)}) collective-permute-start(f32[16,256]{1,0:T(8,128)S(1)} %reduce_sum.40), channel_id=1, source_target_pairs={{0,0},{1,16},{2,32},{3,48},{4,64},{5,80},{6,96},{7,112},{8,128},{9... | collective-permute-start | bytes 49160 | tf_op jit(solution)/shard_map/ppermute | solution.py:224
  171.3 34.5 %all-to-all-start.7 = ((f32[16,16,256]{2,1,0:T(8,128)}), f32[16,16,256]{2,1,0:T(8,128)S(1)}, u32[]{:S(2)}, u32[]{:S(2)}) async-start(f32[16,16,256]{2,1,0:T(8,128)} %broadcast_in_dim.73), calls=%async_computation.7 | async-start | bytes 524288 | tf_op jit(solution)/shard_map/all_to_all | solution.py:38
  207.1 29.4 %all-to-all-start.8 = ((f32[16,48,256]{2,1,0:T(8,128)}), f32[16,48,256]{2,1,0:T(8,128)S(1)}, u32[]{:S(2)}, u32[]{:S(2)}) async-start(f32[16,48,256]{2,1,0:T(8,128)} %pad_maximum_fusion), calls=%async_computation.8 | async-start | bytes 1572864 | tf_op jit(solution)/shard_map/all_to_all | solution.py:38
  238.4 5.4 %copy-start.1 = (f32[256,256]{1,0:T(8,128)S(1)}, f32[256,256]{1,0:T(8,128)}, u32[]{:S(2)}) copy-start(f32[256,256]{1,0:T(8,128)} %shard_map.20) | copy-start | bytes 786436
  238.4 18.1 %all-to-all-start.9 = ((f32[4,272,256]{2,1,0:T(8,128)}), f32[4,272,256]{2,1,0:T(8,128)S(1)}, u32[]{:S(2)}, u32[]{:S(2)}) async-start(f32[4,272,256]{2,1,0:T(8,128)} %broadcast_in_dim.75), calls=%async_computation.9 | async-start | bytes 2228224 | tf_op jit(solution)/shard_map/all_to_all | solution.py:38
  257.2 16.6 %all-to-all-start.10 = ((f32[16,16,256]{2,1,0:T(8,128)}), f32[16,16,256]{2,1,0:T(8,128)}, u32[]{:S(2)}, u32[]{:S(2)}) async-start(f32[16,16,256]{2,1,0:T(8,128)} %broadcast_in_dim.76), calls=%async_computation.10 | async-start | bytes 524288 | tf_op jit(solution)/shard_map/all_to_all | solution.py:38
  264.3 11.5 %copy-start.2 = (f32[256,256]{1,0:T(8,128)S(1)}, f32[256,256]{1,0:T(8,128)}, u32[]{:S(2)}) copy-start(f32[256,256]{1,0:T(8,128)} %bitcast_add_fusion) | copy-start | bytes 786436
  264.3 11.5 %copy-start.4 = (f32[256,256]{1,0:T(8,128)S(1)}, f32[256,256]{1,0:T(8,128)}, u32[]{:S(2)}) copy-start(f32[256,256]{1,0:T(8,128)} %fusion.11) | copy-start | bytes 786436

commit v7 on v6

--- a/solution.py
+++ b/solution.py
@@ -43,24 +43,47 @@
     return exchange(jnp.broadcast_to(piece[None], (n, *piece.shape)), axis)
 
 
+GROUP = 4
+
+
 def invert_half(m_ref, c_ref):
     n = m_ref.shape[0]
     lanes = lax.broadcasted_iota(jnp.int32, (n, n), 1)
     subs = lax.broadcasted_iota(jnp.int32, (n, n), 0)
     lane_row = lax.broadcasted_iota(jnp.int32, (1, n), 1)
 
-    def step(k, carry):
+    def step(trip, carry):
+        k = trip * GROUP
         m = m_ref[...]
-        hit = lanes == k
-        col = jnp.sum(jnp.where(hit, m, 0.0), axis=1, keepdims=True)
-        c_ref[...] = jnp.broadcast_to(col, (n, n))
-        pivot = c_ref[pl.ds(k, 1), :]
-        row = jnp.where(lane_row == k, 1.0, m_ref[pl.ds(k, 1), :]) / pivot
-        rest = jnp.where(hit, 0.0, m) - c_ref[...] * row
-        m_ref[...] = jnp.where(subs == k, row, rest)
+        cols, rows, used = [], [], []
+        for j in range(GROUP):
+            col = jnp.sum(jnp.where(lanes == k + j, m, 0.0), axis=1, keepdims=True)
+            cols.append(jnp.broadcast_to(col, (n, n)))
+            c_ref[j] = cols[j]
+            rows.append(m_ref[pl.ds(k + j, 1), :])
+        for j in range(GROUP):
+            pivot = c_ref[j, pl.ds(k + j, 1), :]
+            row = jnp.where(lane_row == k + j, 1.0, rows[j]) / pivot
+            for i in range(GROUP):
+                if i != j:
+                    factor = c_ref[j, pl.ds(k + i, 1), :]
+                    rows[i] = jnp.where(lane_row == k + j, 0.0, rows[i]) - factor * row
+            rows[j] = row
+            for i in range(j + 1, GROUP):
+                entry = c_ref[i, pl.ds(k + j, 1), :] / pivot
+                cols[i] = jnp.where(subs == k + j, entry, cols[i] - cols[j] * entry)
+                c_ref[i] = cols[i]
+            later = jnp.logical_and(lane_row > k + j, lane_row < k + GROUP)
+            used.append(jnp.where(later, 0.0, row))
+        rest = jnp.where(jnp.logical_and(lanes >= k, lanes < k + GROUP), 0.0, m)
+        for j in range(GROUP):
+            rest = rest - cols[j] * used[j]
+        m_ref[...] = rest
+        for j in range(GROUP):
+            m_ref[pl.ds(k + j, 1), :] = rows[j]
         return carry
 
-    lax.fori_loop(0, n, step, 0)
+    lax.fori_loop(0, n // GROUP, step, 0)
 
 
 def first_half(a_ref, t11_ref, right_ref, left_ref, schur_ref, m_ref, c_ref):
@@ -95,7 +118,10 @@
     return pl.pallas_call(
         first_half,
         out_shape=[half] * 4,
-        scratch_shapes=[pltpu.VMEM(half.shape, jnp.float32)] * 2,
+        scratch_shapes=[
+            pltpu.VMEM(half.shape, jnp.float32),
+            pltpu.VMEM((GROUP, *half.shape), jnp.float32),
+        ],
         cost_estimate=COST,
     )(a)
 
@@ -105,12 +131,12 @@
     return pl.pallas_call(
         second_half,
         out_shape=jax.ShapeDtypeStruct((2 * h, 2 * h), jnp.float32),
-        scratch_shapes=[pltpu.VMEM((h, h), jnp.float32)] * 2,
+        scratch_shapes=[
+            pltpu.VMEM((h, h), jnp.float32),
+            pltpu.VMEM((GROUP, h, h), jnp.float32),
+        ],
         cost_estimate=COST,
     )(*parts)
-
-
-GROUP = 4
 
 
 def eliminate(m_ref, c_ref, u_ref):
@@ -264,13 +290,14 @@
 
     x_part = tn(matrix, refl_r, fast)
     x_piece = jnp.sum(exchange(x_part.reshape(rows, part, width), ROW), axis=0)
-    x_z = to_all(to_block_row(x_piece), "z").reshape(zs * part, width)
+    x_moved, parts = lax.optimization_barrier((to_block_row(x_piece), parts))
+    x_z = to_all(x_moved, "z").reshape(zs * part, width)
+    x_z, parts = lax.optimization_barrier((x_z, parts))
 
     y_part = tn(refl_z, x_z, fast)
     own = jnp.concatenate([x_piece, piece], axis=0)
     own = jnp.broadcast_to(own[None], (rows, 2 * part, width))
     both = jnp.concatenate([own, y_part.reshape(rows, part, width)], axis=1)
-    both, parts = lax.optimization_barrier((both, parts))
     both = exchange(both, ROW)
     tfac = inverted(parts)
     x_c = both[:, :part].reshape(width, width)

time: 279 us -> 281 us (level)
  waiting for transfers between devices: 62.8 us -> 88.5 us
  blocking collectives: 56.6 us -> 31.7 us
  starting transfers between devices: 76.5 us -> 88 us
  Pallas kernels: 54.9 us -> 44.4 us
    all_to_all x8 -> x9, waiting for transfers between devices: 53.9 us -> 83.1 us  [exchange(): return lax.all_to_all(tiles, axis, 0, 0, tiled=True)]
    all_to_all x3 -> x2, blocking collectives: 56.6 us -> 31.7 us  [exchange(): return lax.all_to_all(tiles, axis, 0, 0, tiled=True)]
    all_to_all x8 -> x9, starting transfers between devices: 67.5 us -> 79 us  [exchange(): return lax.all_to_all(tiles, axis, 0, 0, tiled=True)]
    pallas_call x1, Pallas kernels: 16.5 us -> 11.2 us  [inverted(): pl.pallas_call(second_half, out_shape=jax.ShapeDtypeStruct((2 * h, 2 * h)...]
    pallas_call x1, Pallas kernels: 16.4 us -> 11.2 us  [half_inverted(): pl.pallas_call(first_half, out_shape=[half] * 4, scratch_shapes=[pltpu.VM...]
    ppermute x2, waiting for transfers between devices: 8.89 us -> 5.42 us  [to_block_row(): return lax.ppermute(piece, EVERY, pairs)]
  transfers between devices with their start and end apart: 10 -> 11, of which waited for: 8 -> 9; matrix products, arithmetic and copies ran while one was open for 3% -> 3% of each run, Pallas kernels for 20% -> 16%
where the time goes in v7:
time: 281 us; the launch traced here: 279 us
  waiting for transfers between devices  88.5 us (31%)
  starting transfers between devices  88 us (31%)
  Pallas kernels  44.4 us (16%)
  blocking collectives  31.7 us (11%)
  matrix products  14.7 us (5%)
  local copies, waits for them, and re-layouts  6.24 us (2%)
  other arithmetic  5.41 us (2%)
    all_to_all x9, waiting for transfers between devices, exchange(): return lax.all_to_all(tiles, axis, 0, 0, tiled=True)  83.1 us
    all_to_all x9, starting transfers between devices, exchange(): return lax.all_to_all(tiles, axis, 0, 0, tiled=True)  79 us
    all_to_all x2, blocking collectives, exchange(): return lax.all_to_all(tiles, axis, 0, 0, tiled=True)  31.7 us
    dot_general x12, matrix products, dot(): lax.dot_general(left, right, (dims, ((), ())), precision=precision, prefe...  14.7 us
    pallas_call x1, Pallas kernels, half_factored(): pl.pallas_call(first_rows, out_shape=[jax.ShapeDtypeStruct((h, n), jnp.fl...  11.4 us
    pallas_call x1, Pallas kernels, inverted(): pl.pallas_call(second_half, out_shape=jax.ShapeDtypeStruct((2 * h, 2 * h)...  11.2 us
    pallas_call x1, Pallas kernels, half_inverted(): pl.pallas_call(first_half, out_shape=[half] * 4, scratch_shapes=[pltpu.VM...  11.2 us
    pallas_call x1, Pallas kernels, factored(): pl.pallas_call(last_rows, out_shape=jax.ShapeDtypeStruct((n, n), jnp.floa...  10.5 us
  transfers between devices with their start and end apart: 11, of which 9 were waited for; matrix products, arithmetic and copies ran while one was open for 3% of the time, Pallas kernels for 16%

profile of v7, /device:TPU:1, one launch (start us, length us, event | category | flops | bytes accessed | tf_op | source)
XLA Modules:
  0.0 279.4 jit_solution(10714273122937226417)
XLA Ops:
  4.5 17.5 %all-to-all-start = ((f32[16,32,256]{2,1,0:T(8,128)}), f32[16,32,256]{2,1,0:T(8,128)S(1)}, u32[]{:S(2)}, u32[]{:S(2)}) async-start(f32[16,32,256]{2,1,0:T(8,128)} %pad_maximum_fusion.1), calls=%async_computation | async-start | bytes 1048576 | tf_op jit(solution)/shard_map/all_to_all | solution.py:38
  22.0 17.3 %all-to-all-done = f32[16,32,256]{2,1,0:T(8,128)S(1)} async-done(((f32[16,32,256]{2,1,0:T(8,128)}), f32[16,32,256]{2,1,0:T(8,128)S(1)}, u32[]{:S(2)}, u32[]{:S(2)}) %all-to-all-start) | async-done | bytes 524320 | tf_op jit(solution)/shard_map/all_to_all | solution.py:38
  39.3 6.8 %all_to_all.55 = f32[4,16,256]{2,1,0:T(8,128)S(1)} all-to-all(f32[4,16,256]{2,1,0:T(8,128)S(1)} %broadcast_in_dim.32), channel_id=1, replica_groups=mesh['y'=8,'core'=2,'x'=4,'z'=16] {'x'}, dimensions={0} | all-to-all | bytes 131072 | tf_op jit(solution)/shard_map/lead_x/all_to_all | solution.py:38
  46.2 24.9 %all_to_all.56 = f32[16,16,256]{2,1,0:T(8,128)S(1)} all-to-all(f32[16,16,256]{2,1,0:T(8,128)S(1)} %broadcast_in_dim.34), channel_id=1, replica_groups=mesh['y'=8,'core'=2,'x'=4,'z'=16] {'z'}, dimensions={0} | all-to-all | bytes 524288 | tf_op jit(solution)/shard_map/all_to_all | solution.py:38
  71.9 8.5 %all-to-all-start.3 = ((f32[16,32,256]{2,1,0:T(8,128)}), f32[16,32,256]{2,1,0:T(8,128)S(1)}, u32[]{:S(2)}, u32[]{:S(2)}) async-start(f32[16,32,256]{2,1,0:T(8,128)} %broadcast_in_dim.70), calls=%async_computation.3 | async-start | bytes 1048576 | tf_op jit(solution)/shard_map/all_to_all | solution.py:38
  80.4 3.5 %collective-permute-start = (f32[16,256]{1,0:T(8,128)S(1)}, f32[16,256]{1,0:T(8,128)S(1)}, u32[]{:S(2)}, u32[]{:S(2)}) collective-permute-start(f32[16,256]{1,0:T(8,128)S(1)} %get-tuple-element.60), channel_id=1, source_target_pairs={{0,0},{1,16},{2,32},{3,48},{4,64},{5,80},{6,96},{7,112},{8,128},{9... | collective-permute-start | bytes 49160 | tf_op jit(solution)/shard_map/move_panel/ppermute | solution.py:250
  84.0 5.4 %collective-permute-done = f32[16,256]{1,0:T(8,128)S(1)} collective-permute-done((f32[16,256]{1,0:T(8,128)S(1)}, f32[16,256]{1,0:T(8,128)S(1)}, u32[]{:S(2)}, u32[]{:S(2)}) %collective-permute-start) | collective-permute-done | bytes 16416 | tf_op jit(solution)/shard_map/move_panel/ppermute | solution.py:250
  89.4 8.4 %all-to-all-done.3 = f32[16,32,256]{2,1,0:T(8,128)S(1)} async-done(((f32[16,32,256]{2,1,0:T(8,128)}), f32[16,32,256]{2,1,0:T(8,128)S(1)}, u32[]{:S(2)}, u32[]{:S(2)}) %all-to-all-start.3) | async-done | bytes 524320 | tf_op jit(solution)/shard_map/all_to_all | solution.py:38
  98.5 7.2 %all-to-all-start.4 = ((f32[16,16,256]{2,1,0:T(8,128)}), f32[16,16,256]{2,1,0:T(8,128)S(1)}, u32[]{:S(2)}, u32[]{:S(2)}) async-start(f32[16,16,256]{2,1,0:T(8,128)} %broadcast_in_dim.71), calls=%async_computation.4 | async-start | bytes 524288 | tf_op jit(solution)/shard_map/all_to_all | solution.py:38
  106.4 11.4 %shard_map.17 = (f32[128,256]{1,0:T(8,128)}, f32[128,128]{1,0:T(8,128)}) custom-call(f32[256,256]{1,0:T(8,128)} %bitcast.57), custom_call_target="tpu_custom_call" | custom-call | flops 2000000000 | bytes 500000 | tf_op jit(solution)/shard_map/pallas_call | solution.py:213
  124.1 10.5 %shard_map.18 = f32[256,256]{1,0:T(8,128)} custom-call(f32[128,256]{1,0:T(8,128)} %get-tuple-element.35.rows_ref, f32[128,128]{1,0:T(8,128)} %get-tuple-element.36.schur_ref), custom_call_target="tpu_custom_call" | custom-call | flops 2000000000 | bytes 500000 | tf_op jit(solution)/shard_map/pallas_call | solution.py:227
  137.3 13.4 %all-to-all-start.6 = ((f32[16,16,256]{2,1,0:T(8,128)}), f32[16,16,256]{2,1,0:T(8,128)S(1)}, u32[]{:S(2)}, u32[]{:S(2)}) async-start(f32[16,16,256]{2,1,0:T(8,128)} %bitcast.12), calls=%async_computation.6 | async-start | bytes 524288 | tf_op jit(solution)/shard_map/all_to_all | solution.py:38
  152.0 10.3 %all-to-all-done.6 = f32[16,16,256]{2,1,0:T(8,128)S(1)} async-done(((f32[16,16,256]{2,1,0:T(8,128)}), f32[16,16,256]{2,1,0:T(8,128)S(1)}, u32[]{:S(2)}, u32[]{:S(2)}) %all-to-all-start.6) | async-done | bytes 262176 | tf_op jit(solution)/shard_map/all_to_all | solution.py:38
  162.3 5.5 %collective-permute-start.1 = (f32[16,256]{1,0:T(8,128)S(1)}, f32[16,256]{1,0:T(8,128)S(1)}, u32[]{:S(2)}, u32[]{:S(2)}) collective-permute-start(f32[16,256]{1,0:T(8,128)S(1)} %reduce_sum.40), channel_id=1, source_target_pairs={{0,0},{1,16},{2,32},{3,48},{4,64},{5,80},{6,96},{7,112},{8,128},{9... | collective-permute-start | bytes 49160 | tf_op jit(solution)/shard_map/ppermute | solution.py:250
  167.8 11.2 %shard_map.19 = (f32[128,128]{1,0:T(8,128)}, f32[128,128]{1,0:T(8,128)}, f32[128,128]{1,0:T(8,128)}, f32[128,128]{1,0:T(8,128)}) custom-call(f32[256,256]{1,0:T(8,128)} %convolution_add_fusion.a_ref), custom_call_target="tpu_custom_call" | custom-call | flops 2000000000 | bytes 500000 | tf_op jit(solution)/shard_map/pallas_call | solution.py:118
  179.8 10.2 %all-to-all-start.7 = ((f32[16,16,256]{2,1,0:T(8,128)}), f32[16,16,256]{2,1,0:T(8,128)S(1)}, u32[]{:S(2)}, u32[]{:S(2)}) async-start(f32[16,16,256]{2,1,0:T(8,128)} %broadcast_in_dim.73), calls=%async_computation.7 | async-start | bytes 524288 | tf_op jit(solution)/shard_map/all_to_all | solution.py:38
  190.0 13.8 %all-to-all-done.7 = f32[16,16,256]{2,1,0:T(8,128)S(1)} async-done(((f32[16,16,256]{2,1,0:T(8,128)}), f32[16,16,256]{2,1,0:T(8,128)S(1)}, u32[]{:S(2)}, u32[]{:S(2)}) %all-to-all-start.7) | async-done | bytes 262176 | tf_op jit(solution)/shard_map/all_to_all | solution.py:38
  205.1 10.1 %all-to-all-start.8 = ((f32[16,48,256]{2,1,0:T(8,128)}), f32[16,48,256]{2,1,0:T(8,128)S(1)}, u32[]{:S(2)}, u32[]{:S(2)}) async-start(f32[16,48,256]{2,1,0:T(8,128)} %pad_maximum_fusion), calls=%async_computation.8 | async-start | bytes 1572864 | tf_op jit(solution)/shard_map/all_to_all | solution.py:38
  215.2 11.2 %shard_map.20 = f32[256,256]{1,0:T(8,128)} custom-call(f32[128,128]{1,0:T(8,128)} %get-tuple-element.49.t11_ref, f32[128,128]{1,0:T(8,128)} %get-tuple-element.50.right_ref, f32[128,128]{1,0:T(8,128)} %get-tuple-element.51.left_ref, f32[128,128]{1,0:T(8,128)} %get-tuple-element.52.schur_ref), custom_call_target="tpu_custom_call" | custom-call | flops 2000000000 | bytes 500000 | tf_op jit(solution)/shard_map/pallas_call | solution.py:131
  226.5 11.5 %all-to-all-done.8 = f32[16,48,256]{2,1,0:T(8,128)S(1)} async-done(((f32[16,48,256]{2,1,0:T(8,128)}), f32[16,48,256]{2,1,0:T(8,128)S(1)}, u32[]{:S(2)}, u32[]{:S(2)}) %all-to-all-start.8) | async-done | bytes 786464 | tf_op jit(solution)/shard_map/all_to_all | solution.py:38
  239.9 3.7 %all-to-all-start.9 = ((f32[4,272,256]{2,1,0:T(8,128)}), f32[4,272,256]{2,1,0:T(8,128)S(1)}, u32[]{:S(2)}, u32[]{:S(2)}) async-start(f32[4,272,256]{2,1,0:T(8,128)} %broadcast_in_dim.75), calls=%async_computation.9 | async-start | bytes 2228224 | tf_op jit(solution)/shard_map/all_to_all | solution.py:38
  247.3 10.7 %all-to-all-done.9 = f32[4,272,256]{2,1,0:T(8,128)S(1)} async-done(((f32[4,272,256]{2,1,0:T(8,128)}), f32[4,272,256]{2,1,0:T(8,128)S(1)}, u32[]{:S(2)}, u32[]{:S(2)}) %all-to-all-start.9) | async-done | bytes 1114144 | tf_op jit(solution)/shard_map/all_to_all | solution.py:38
  258.8 5.0 %all-to-all-start.10 = ((f32[16,16,256]{2,1,0:T(8,128)}), f32[16,16,256]{2,1,0:T(8,128)}, u32[]{:S(2)}, u32[]{:S(2)}) async-start(f32[16,16,256]{2,1,0:T(8,128)} %broadcast_in_dim.76), calls=%async_computation.10 | async-start | bytes 524288 | tf_op jit(solution)/shard_map/all_to_all | solution.py:38
  265.8 9.6 %all-to-all-done.10 = f32[16,16,256]{2,1,0:T(8,128)} async-done(((f32[16,16,256]{2,1,0:T(8,128)}), f32[16,16,256]{2,1,0:T(8,128)}, u32[]{:S(2)}, u32[]{:S(2)}) %all-to-all-start.10) | async-done | bytes 262176 | tf_op jit(solution)/shard_map/all_to_all | solution.py:38
  (54 shorter events, 31.5 us)
Async XLA Ops:
  0.0 2.9 %copy-start = (f32[1024,256]{1,0:T(8,128)S(1)}, f32[1024,256]{1,0:T(8,128)}, u32[]{:S(2)}) copy-start(f32[1024,256]{1,0:T(8,128)} %param.1) | copy-start | bytes 3145732
  4.5 34.8 %all-to-all-start = ((f32[16,32,256]{2,1,0:T(8,128)}), f32[16,32,256]{2,1,0:T(8,128)S(1)}, u32[]{:S(2)}, u32[]{:S(2)}) async-start(f32[16,32,256]{2,1,0:T(8,128)} %pad_maximum_fusion.1), calls=%async_computation | async-start | bytes 1048576 | tf_op jit(solution)/shard_map/all_to_all | solution.py:38
  71.9 25.8 %all-to-all-start.3 = ((f32[16,32,256]{2,1,0:T(8,128)}), f32[16,32,256]{2,1,0:T(8,128)S(1)}, u32[]{:S(2)}, u32[]{:S(2)}) async-start(f32[16,32,256]{2,1,0:T(8,128)} %broadcast_in_dim.70), calls=%async_computation.3 | async-start | bytes 1048576 | tf_op jit(solution)/shard_map/all_to_all | solution.py:38
  80.4 9.0 %collective-permute-start = (f32[16,256]{1,0:T(8,128)S(1)}, f32[16,256]{1,0:T(8,128)S(1)}, u32[]{:S(2)}, u32[]{:S(2)}) collective-permute-start(f32[16,256]{1,0:T(8,128)S(1)} %get-tuple-element.60), channel_id=1, source_target_pairs={{0,0},{1,16},{2,32},{3,48},{4,64},{5,80},{6,96},{7,112},{8,128},{9... | collective-permute-start | bytes 49160 | tf_op jit(solution)/shard_map/move_panel/ppermute | solution.py:250
  98.5 21.0 %all-to-all-start.4 = ((f32[16,16,256]{2,1,0:T(8,128)}), f32[16,16,256]{2,1,0:T(8,128)S(1)}, u32[]{:S(2)}, u32[]{:S(2)}) async-start(f32[16,16,256]{2,1,0:T(8,128)} %broadcast_in_dim.71), calls=%async_computation.4 | async-start | bytes 524288 | tf_op jit(solution)/shard_map/all_to_all | solution.py:38
  120.5 14.1 %all-to-all-start.5 = ((f32[4,256,256]{2,1,0:T(8,128)}), f32[4,256,256]{2,1,0:T(8,128)S(1)}, u32[]{:S(2)}, u32[]{:S(2)}) async-start(f32[4,256,256]{2,1,0:T(8,128)} %broadcast_in_dim.72), calls=%async_computation.5 | async-start | bytes 2097152 | tf_op jit(solution)/shard_map/all_to_all | solution.py:38
  135.6 15.1 %copy-start.2 = (f32[256,256]{1,0:T(8,128)S(1)}, f32[256,256]{1,0:T(8,128)}, u32[]{:S(2)}) copy-start(f32[256,256]{1,0:T(8,128)} %shard_map.18) | copy-start | bytes 786436
  135.6 15.1 %copy-start.5 = (f32[16,16,256]{2,1,0:T(8,128)S(1)}, f32[16,16,256]{2,1,0:T(8,128)}, u32[]{:S(2)}) copy-start(f32[16,16,256]{2,1,0:T(8,128)} %get-tuple-element.59) | copy-start | bytes 786436
  137.3 25.0 %all-to-all-start.6 = ((f32[16,16,256]{2,1,0:T(8,128)}), f32[16,16,256]{2,1,0:T(8,128)S(1)}, u32[]{:S(2)}, u32[]{:S(2)}) async-start(f32[16,16,256]{2,1,0:T(8,128)} %bitcast.12), calls=%async_computation.6 | async-start | bytes 524288 | tf_op jit(solution)/shard_map/all_to_all | solution.py:38
  162.3 16.7 %collective-permute-start.1 = (f32[16,256]{1,0:T(8,128)S(1)}, f32[16,256]{1,0:T(8,128)S(1)}, u32[]{:S(2)}, u32[]{:S(2)}) collective-permute-start(f32[16,256]{1,0:T(8,128)S(1)} %reduce_sum.40), channel_id=1, source_target_pairs={{0,0},{1,16},{2,32},{3,48},{4,64},{5,80},{6,96},{7,112},{8,128},{9... | collective-permute-start | bytes 49160 | tf_op jit(solution)/shard_map/ppermute | solution.py:250
  179.8 24.0 %all-to-all-start.7 = ((f32[16,16,256]{2,1,0:T(8,128)}), f32[16,16,256]{2,1,0:T(8,128)S(1)}, u32[]{:S(2)}, u32[]{:S(2)}) async-start(f32[16,16,256]{2,1,0:T(8,128)} %broadcast_in_dim.73), calls=%async_computation.7 | async-start | bytes 524288 | tf_op jit(solution)/shard_map/all_to_all | solution.py:38
  205.1 32.8 %all-to-all-start.8 = ((f32[16,48,256]{2,1,0:T(8,128)}), f32[16,48,256]{2,1,0:T(8,128)S(1)}, u32[]{:S(2)}, u32[]{:S(2)}) async-start(f32[16,48,256]{2,1,0:T(8,128)} %pad_maximum_fusion), calls=%async_computation.8 | async-start | bytes 1572864 | tf_op jit(solution)/shard_map/all_to_all | solution.py:38
  239.9 5.4 %copy-start.1 = (f32[256,256]{1,0:T(8,128)S(1)}, f32[256,256]{1,0:T(8,128)}, u32[]{:S(2)}) copy-start(f32[256,256]{1,0:T(8,128)} %shard_map.20) | copy-start | bytes 786436
  239.9 18.1 %all-to-all-start.9 = ((f32[4,272,256]{2,1,0:T(8,128)}), f32[4,272,256]{2,1,0:T(8,128)S(1)}, u32[]{:S(2)}, u32[]{:S(2)}) async-start(f32[4,272,256]{2,1,0:T(8,128)} %broadcast_in_dim.75), calls=%async_computation.9 | async-start | bytes 2228224 | tf_op jit(solution)/shard_map/all_to_all | solution.py:38
  258.8 16.6 %all-to-all-start.10 = ((f32[16,16,256]{2,1,0:T(8,128)}), f32[16,16,256]{2,1,0:T(8,128)}, u32[]{:S(2)}, u32[]{:S(2)}) async-start(f32[16,16,256]{2,1,0:T(8,128)} %broadcast_in_dim.76), calls=%async_computation.10 | async-start | bytes 524288 | tf_op jit(solution)/shard_map/all_to_all | solution.py:38
  265.8 11.5 %copy-start.3 = (f32[256,256]{1,0:T(8,128)S(1)}, f32[256,256]{1,0:T(8,128)}, u32[]{:S(2)}) copy-start(f32[256,256]{1,0:T(8,128)} %bitcast_add_fusion) | copy-start | bytes 786436
  265.8 11.5 %copy-start.4 = (f32[256,256]{1,0:T(8,128)S(1)}, f32[256,256]{1,0:T(8,128)}, u32[]{:S(2)}) copy-start(f32[256,256]{1,0:T(8,128)} %fusion.16) | copy-start | bytes 786436
